TPU v7x, 32 devices: a whole 2x2x4 slice. The times are simulated.
32 devices in a mesh: groups: 2 (over y), gx: 4 (over z), gy: 2 (over x), gz: 2 (over core).
Axes of the slice: x: 2, y: 2, z: 4, core: 2. Of those that a mesh axis runs over, the one named last changes fastest.
Arguments:
- pair: float32 [256, 48, 48], P(('groups', 'gz'), 'gx', 'gy'), parts along dimension 0, may hold values from -6 to 6
- residue_mask: int32 [96], P('groups'), parts along dimension 0, may hold values 0 or 1
- norm_in_gain: float32 [2, 128], P(None, 'gz'), may hold values from 0.25 to 1.75
- proj_weight: bfloat16 [2, 4, 128, 128], P(None, None, None, 'gz'), may hold values from -0.5 to 0.5
- gate_weight: bfloat16 [2, 128, 128], P(None, None, 'gz'), may hold values from -0.5 to 0.5
- norm_out_gain: float32 [2, 128], P(None, 'gz'), may hold values from 0.25 to 1.75
- out_weight: bfloat16 [2, 128, 128], P(None, None, 'gz'), may hold values from -0.5 to 0.5
Outputs:
- pair_out: float32 [256, 48, 48], P(('groups', 'gz'), 'gx', 'gy'), parts along dimension 0
There are 2 independent parts, one for each index of `groups`. A program takes and returns all parts, laid end to end along the dimension named above; an argument that names none is the same for every part. Nothing has to cross between parts.
All inputs are finite; a program needn't handle non-finite values.
Results may differ from a plain program's by a relative error of at most 0.006.
Values may be sent and summed in bfloat16 or wider, within the bound.
No kernel may reach another device: no remote copies, remote signals or barrier semaphores. Data moves between devices by JAX's collectives and lax.ppermute only.
A program may use at most 64 MiB of HBM per device.

v0:
```python
import functools

import jax
import jax.numpy as jnp
from jax import lax
from jax.experimental import pallas as pl
from jax.experimental.pallas import tpu as pltpu
from jax.sharding import PartitionSpec as P


EPSILON = 1e-05
F32 = jnp.float32
BF16 = jnp.bfloat16
REPLICATED_LIMIT = 4 * 1024 * 1024


def dot(x, w):
    return jnp.dot(x.astype(BF16), w, preferred_element_type=F32)


def lane_norm(x, gain, ones):
    d = x - jnp.mean(x, axis=-1, keepdims=True)
    return d * lax.rsqrt(dot(d * d, ones) + EPSILON) * gain


def gated(x, w):
    p = dot(x, w)
    ch = p.shape[1] // 2
    return (jnp.tanh(p[:, :ch]) + 1.0) * p[:, ch:]


def rows_at(first, count):
    return pl.ds(first if isinstance(first, int) else pl.multiple_of(first, 8), count)


def own_kernel(tile, out):
    half = tile.shape[0] // 2
    rows = tile[pl.ds(lax.axis_index("gz") * half, half)]
    out[...] = rows.reshape(out.shape)


def centre_kernel(own, other, out):
    core = lax.axis_index("gz")
    pairs, part = own.shape
    half = other.shape[0] // 2
    theirs = other[pl.ds(core * half, half)].reshape(pairs, part)
    both = pltpu.roll(jnp.concatenate([own[...], theirs], axis=1), core * part, 1)
    out[...] = (both - jnp.mean(both, axis=-1, keepdims=True)).astype(BF16)


def weights_kernel(own, other, own_gains, other_gains, flags, wleft, wright, wgate, wout, gains, mask):
    core = lax.axis_index("gz")
    half = own.shape[2]
    for u in range(2):
        for p in range(6):
            mine, theirs = own[u, p].astype(F32) * 0.5, other[u, p].astype(F32) * 0.5
            first = jnp.where(core == 0, mine, theirs)
            second = jnp.where(core == 0, theirs, mine)
            full = jnp.transpose(jnp.concatenate([first, second], axis=0)).astype(BF16)
            if p < 2:
                wleft[u, :, p * 2 * half : (p + 1) * 2 * half] = full
            elif p < 4:
                wright[u, :, (p - 2) * 2 * half : (p - 1) * 2 * half] = full
            elif p == 4:
                wgate[u] = full
            else:
                wout[u] = full
    gains[...] = pltpu.roll(jnp.concatenate([own_gains[...], other_gains[...]], axis=1), core * half, 1)
    row = flags[...].astype(F32)
    size = row.shape[1]
    wide = jnp.transpose(jnp.broadcast_to(row, (mask.shape[1], size)))
    mask[...] = jnp.zeros_like(mask)
    mask[:size, :] = wide


class Place:
    def __init__(self, res, tile_rows, tile_cols):
        self.res, self.rows, self.cols = res, tile_rows, tile_cols
        self.half = tile_rows // 2
        self.ipad = -(-tile_rows // 8) * 8
        self.span = tile_cols + self.ipad
        self.row_block = lax.axis_index("gx")
        self.col_block = lax.axis_index("gy")
        self.core = lax.axis_index("gz")
        self.first_row = self.row_block * tile_rows
        self.first_col = self.col_block * tile_cols


def column_phase(at, own, other, mask, gains, wleft, wright, raw, normed, left, rightt, column):
    ch = mask.shape[1]
    cols, span = at.cols, at.span
    for s in range(own.shape[0]):
        for source, which in ((own, at.core), (other, 1 - at.core)):
            x = source[s].astype(F32)
            var = jnp.mean(x * x, axis=-1, keepdims=True)
            first = ((at.row_block ^ s) * at.rows + which * at.half) * cols
            where = pl.ds(pl.multiple_of(first, 8), at.half * cols)
            raw[where, :] = x
            normed[where, :] = x * lax.rsqrt(var + EPSILON) * gains[0:1, :]
    pairs = at.res * cols
    raw[pairs:, :] = jnp.zeros((raw.shape[0] - pairs, ch), F32)
    normed[pairs:, :] = jnp.zeros((raw.shape[0] - pairs, ch), F32)

    kmask = mask[rows_at(column * cols, cols), :]
    y = gated(normed[:pairs, :], wleft[0]).reshape(at.res, cols, ch) * kmask[None]
    left[...] = y.reshape(pairs, ch)

    for k in range(at.ipad - at.rows):
        rightt[pl.ds(cols + at.rows + k, cols, stride=span), :] = jnp.zeros((cols, ch), F32)
    for slot in range(0, cols + at.rows, at.rows):
        row = at.first_col + slot if slot < cols else at.first_row
        y = gated(normed[rows_at(row * cols, at.rows * cols), :], wright[0])
        for q in range(at.rows):
            rightt[pl.ds(slot + q, cols, stride=span), :] = y[q * cols : (q + 1) * cols]


def triangle_phase(at, left, rightt, tri, start):
    cols, span = at.cols, at.span
    ch = left.shape[1]
    count = 4

    def tri_block(n, carry):
        first = n * count

        def add(k, accs):
            r = rightt[pl.ds(pl.multiple_of(k * span, 8), span), :]
            return tuple(acc + left[pl.ds((first + q) * cols + k, 1), :] * r for q, acc in enumerate(accs))

        where = [pl.ds(pl.multiple_of((first + q) * span, 8), span) for q in range(count)]
        accs = tuple(jnp.zeros((span, ch), F32) if start is None else start[w, :] for w in where)
        accs = lax.fori_loop(0, cols, add, accs, unroll=min(cols, 24))
        for w, acc in zip(where, accs):
            tri[w, :] = acc
        return carry

    lax.fori_loop(0, at.res // count, tri_block, 0)


def near_kernel(own, other, mask, gains, wleft, wright, raw, normed, left, rightt, *, place):
    at = Place(*place)
    column_phase(at, own, other, mask, gains, wleft, wright, raw, normed, left, rightt, at.col_block)


def near_triangle_kernel(left, rightt, tri, *, place):
    triangle_phase(Place(*place), left, rightt, tri, None)


def far_kernel(
    own, other, near_raw, near_normed, near_tri, mask, gains, wleft, wright, wgate, wout, pair, out,
    raw, normed, left, rightt, tri, first_update, znext, right1, left1, *, place,
):
    at = Place(*place)
    res, rows, cols, ipad, span = at.res, at.rows, at.cols, at.ipad, at.span
    ch = mask.shape[1]
    column_phase(at, own, other, mask, gains, wleft, wright, raw, normed, left, rightt, 1 - at.col_block)
    triangle_phase(at, left, rightt, tri, near_tri)
    ones = jnp.full((ch, ch), 1.0 / ch, BF16)
    gain_in, gain_out = gains[0:2, :], gains[2:4, :]

    smask = jnp.concatenate(
        [mask[rows_at(at.first_col, cols), :], mask[pl.ds(at.first_row, ipad), :]], axis=0
    )
    row_is_near = at.first_row // cols == at.col_block
    offset = at.first_row % cols
    zs, ns, ms = [], [], []
    for r in range(res):
        where = pl.ds(r * cols + offset, ipad)
        zs += [near_raw[r * cols : (r + 1) * cols, :], jnp.where(row_is_near, near_raw[where, :], raw[where, :])]
        ns += [
            near_normed[r * cols : (r + 1) * cols, :],
            jnp.where(row_is_near, near_normed[where, :], normed[where, :]),
        ]
        ms.append(smask * mask[r : r + 1, :])
    gate = jnp.tanh(dot(jnp.concatenate(ns, axis=0), wgate[0])) + 1.0
    tn = lane_norm(tri[...], gain_out[0:1], ones)
    update = gate * dot(tn, wout[0]) * jnp.concatenate(ms, axis=0)
    first_update[...] = update
    znext[...] = lane_norm(jnp.concatenate(zs, axis=0) + update, gain_in[1:2], ones)

    z3 = znext[...].reshape(res, span, ch)
    right1[...] = gated(z3[:, :cols].reshape(res * cols, ch), wright[1])
    v = gated(z3[:, cols:].reshape(res * ipad, ch), wleft[1]).reshape(res, ipad, ch) * mask[:res, :][:, None, :]
    left1[...] = v.reshape(res * ipad, ch)

    def tri1_block(k, accs):
        r = right1[pl.ds(pl.multiple_of(k * cols, 8), cols), :]
        return tuple(acc + left1[pl.ds(k * ipad + i, 1), :] * r for i, acc in enumerate(accs))

    accs = lax.fori_loop(0, res, tri1_block, tuple(jnp.zeros((cols, ch), F32) for _ in range(rows)), unroll=4)
    tn = lane_norm(jnp.concatenate(accs, axis=0), gain_out[1:2], ones)
    ns, us, ms = [], [], []
    for i in range(rows):
        where = pl.ds(pl.multiple_of((at.first_row + i) * span, 8), cols)
        ns.append(znext[where, :])
        us.append(first_update[where, :])
        ms.append(smask[:cols] * mask[pl.ds(at.first_row + i, 1), :])
    gate = jnp.tanh(dot(jnp.concatenate(ns, axis=0), wgate[1])) + 1.0
    update = gate * dot(tn, wout[1]) * jnp.concatenate(ms, axis=0)
    moved = jnp.concatenate(us, axis=0) + update
    part = ch // 2
    moved = pltpu.roll(moved, at.core * part, 1)[:, :part]
    out[...] = pair[...] + moved.reshape(rows, cols, part)


def swap(x, axis, mask=1):
    size = lax.axis_size(axis)
    return lax.ppermute(x, axis, [(i, i ^ mask) for i in range(size)])


def call(kernel, out_shape, *args, scratch=(), vmem_mib=4, flops=2**20):
    return pl.pallas_call(
        kernel,
        out_shape=out_shape,
        scratch_shapes=list(scratch),
        compiler_params=pltpu.CompilerParams(vmem_limit_bytes=vmem_mib * 1024 * 1024),
        cost_estimate=pl.CostEstimate(flops=flops, bytes_accessed=2**16, transcendentals=0),
    )(*args)


def replicated(
    pair, residue_mask, norm_in_gain, proj_weight, gate_weight, norm_out_gain, out_weight
):
    part, tile_rows, tile_cols = pair.shape
    tile = jnp.transpose(pair, (1, 2, 0))
    res = residue_mask.shape[0]
    ch = 2 * part
    half = tile_rows // 2
    ipad = -(-tile_rows // 8) * 8
    span = tile_cols + ipad
    blocks = lax.axis_size("gx")
    place = (res, tile_rows, tile_cols)
    pairs = res * tile_cols
    wide = lambda rows: jax.ShapeDtypeStruct((rows, ch), F32)
    vmem = lambda rows: pltpu.VMEM((rows, ch), F32)
    narrow = lambda *shape: jax.ShapeDtypeStruct(shape, BF16)

    other_tile = swap(tile, "gz")
    own_weights = jnp.concatenate(
        [
            jnp.transpose(proj_weight, (0, 1, 3, 2)),
            jnp.transpose(gate_weight, (0, 2, 1))[:, None],
            jnp.transpose(out_weight, (0, 2, 1))[:, None],
        ],
        axis=1,
    )
    own_gains = jnp.concatenate([norm_in_gain, norm_out_gain], axis=0)
    other_weights = swap(own_weights, "gz")
    other_gains = swap(own_gains, "gz")

    own_rows = call(own_kernel, jax.ShapeDtypeStruct((half * tile_cols, part), F32), tile)
    message = call(centre_kernel, narrow(half * tile_cols, ch), own_rows, other_tile)
    column = [message]
    for s in range(1, blocks):
        column.append(swap(message, "gx", s))
    wleft, wright, wgate, wout, gains, mask = call(
        weights_kernel,
        [narrow(2, ch, 2 * ch), narrow(2, ch, 2 * ch), narrow(2, ch, ch), narrow(2, ch, ch), wide(4), wide(res + 8)],
        own_weights, other_weights, own_gains, other_gains, residue_mask[None, :],
        vmem_mib=8,
    )
    near = jnp.stack(column)
    far = swap(near, "gy")
    near_other = swap(near, "gz")
    far_other = swap(far, "gz")
    near_raw, near_normed, near_left, near_right = call(
        functools.partial(near_kernel, place=place),
        [wide(pairs + 8), wide(pairs + 8), wide(pairs), wide(tile_cols * span)],
        near, near_other, mask, gains, wleft, wright,
        flops=2**26,
    )
    near_tri = call(
        functools.partial(near_triangle_kernel, place=place),
        wide(res * span),
        near_left, near_right,
        flops=2**26,
    )
    result = call(
        functools.partial(far_kernel, place=place),
        jax.ShapeDtypeStruct(tile.shape, F32),
        far, far_other, near_raw, near_normed, near_tri, mask, gains, wleft, wright, wgate, wout, tile,
        scratch=[
            vmem(pairs + 8),
            vmem(pairs + 8),
            vmem(pairs),
            vmem(tile_cols * span),
            vmem(res * span),
            vmem(res * span),
            vmem(res * span),
            vmem(pairs),
            vmem(res * ipad),
        ],
        vmem_mib=24,
    )
    return jnp.transpose(result, (2, 0, 1))


def layer_norm_gathered(values, gain_part):
    full_values, full_gain = (
        lax.all_gather(values, "gz", axis=0, tiled=True),
        lax.all_gather(gain_part, "gz", axis=0, tiled=True),
    )
    mean_val = jnp.mean(full_values, axis=0)
    centred = full_values - mean_val
    spread = jnp.mean(centred * centred, axis=0)
    result = (centred * lax.rsqrt(spread + EPSILON) * full_gain[:, None, None]).astype(jnp.bfloat16)
    return result


def transpose_tile(pair_tile):
    depth_dim, tile_rows, tile_cols = pair_tile.shape
    across = lax.axis_size("gy")
    down_size = lax.axis_size("gx")
    quarter = tile_rows // across
    spread_rows = lax.all_to_all(pair_tile, "gy", split_axis=1, concat_axis=2, tiled=True)
    blocks = spread_rows.reshape(depth_dim, quarter, down_size, tile_rows)
    blocks = jnp.transpose(blocks, (0, 3, 2, 1))[:, :, :, None, :]
    moved_back = lax.all_to_all(
        lax.all_to_all(blocks, "gx", split_axis=2, concat_axis=2, tiled=True),
        "gy",
        split_axis=2,
        concat_axis=3,
        tiled=True,
    )
    return moved_back.reshape(depth_dim, tile_rows, tile_cols)


def fold_panels(left_tile, right_tile):
    left_panel = lax.all_gather(left_tile, "gy", axis=2, tiled=True)
    return jnp.einsum(
        "hik,hkj->hij",
        left_panel,
        lax.all_gather(right_tile, "gx", axis=1, tiled=True),
        preferred_element_type=jnp.float32,
    )


def distributed(
    pair, residue_mask, norm_in_gain, proj_weight, gate_weight, norm_out_gain, out_weight
):
    tile_rows = pair.shape[1]
    tile_cols = pair.shape[2]
    row_start = lax.axis_index("gx") * tile_rows
    col_start = lax.axis_index("gy") * tile_cols
    row_flags = lax.dynamic_slice_in_dim(residue_mask, row_start, tile_rows).astype(jnp.float32)
    col_flags = lax.dynamic_slice_in_dim(residue_mask, col_start, tile_cols).astype(jnp.float32)
    pair_mask = row_flags[:, None] * col_flags[None, :]
    current = pair
    for update in range(2):
        normed = layer_norm_gathered(current, norm_in_gain[update])
        projected = jnp.einsum(
            "cij,pch->phij", normed, proj_weight[update], preferred_element_type=jnp.float32
        )
        left_tile = (jax.nn.sigmoid(projected[0]) * projected[1] * pair_mask).astype(jnp.bfloat16)
        right_tile = (jax.nn.sigmoid(projected[2]) * projected[3] * pair_mask).astype(jnp.bfloat16)
        gate_values = jax.nn.sigmoid(
            jnp.einsum(
                "cij,cd->dij", normed, gate_weight[update], preferred_element_type=jnp.float32
            )
        )
        if update == 0:
            triangle = fold_panels(left_tile, transpose_tile(right_tile))
        else:
            triangle = fold_panels(transpose_tile(left_tile), right_tile)
        tri_normed = layer_norm_gathered(triangle, norm_out_gain[update])
        current = current + gate_values * jnp.einsum(
            "hij,hd->dij", tri_normed, out_weight[update], preferred_element_type=jnp.float32
        )
    return current


def fits_replicated(pair, residue_mask):
    part, tile_rows, tile_cols = pair.shape
    res = residue_mask.shape[0]
    return (
        lax.axis_size("gz") == 2
        and res * res * part * 2 * 4 <= REPLICATED_LIMIT
        and lax.axis_size("gy") == 2
        and lax.axis_size("gx").bit_count() == 1
        and res % 4 == 0
        and tile_rows % 2 == 0
        and tile_cols % 8 == 0
        and tile_cols % tile_rows == 0
    )


def per_device(pair, residue_mask, *parameters):
    plan = replicated if fits_replicated(pair, residue_mask) else distributed
    return plan(pair, residue_mask, *parameters)


def solution(mesh):
    return jax.shard_map(
        per_device,
        mesh=mesh,
        in_specs=(
            P(("groups", "gz"), "gx", "gy"),
            P("groups"),
            P(None, "gz"),
            P(None, None, None, "gz"),
            P(None, None, "gz"),
            P(None, "gz"),
            P(None, None, "gz"),
        ),
        out_specs=P(("groups", "gz"), "gx", "gy"),
        check_vma=False,
    )
```

profile of v0, /device:TPU:0, one launch (start us, length us, event | category | flops | bytes accessed | tf_op | source)
XLA Modules:
  0.0 28.6 jit_solution(3241779249268185388)
XLA Ops:
  0.0 0.5 %collective-permute-start = (f32[12,24,64]{2,1,0:T(8,128)}, f32[12,24,64]{2,1,0:T(8,128)S(1)}, u32[]{:S(2)}, u32[]{:S(2)}) collective-permute-start(f32[12,24,64]{2,1,0:T(8,128)} %bitcast.14), channel_id=1, source_target_pairs={{0,1},{1,0},{2,3},{3,2},{4,5},{5,4},{6,7},{7,6},{8,9},{9,8},{10,11... | collective-permute-start | bytes 221192 | tf_op jit(solution)/shard_map/ppermute | solution.py:207
  0.5 0.0 copy-start
  0.5 0.9 %copy-done = f32[64,12,24]{0,2,1:T(8,128)S(1)} copy-done((f32[64,12,24]{0,2,1:T(8,128)S(1)}, f32[64,12,24]{0,2,1:T(8,128)}, u32[]{:S(2)}) %copy-start) | copy-done | bytes 73752
  1.4 0.3 %collective-permute-done.other = f32[12,24,64]{2,1,0:T(8,128)S(1)} collective-permute-done((f32[12,24,64]{2,1,0:T(8,128)}, f32[12,24,64]{2,1,0:T(8,128)S(1)}, u32[]{:S(2)}, u32[]{:S(2)}) %collective-permute-start) | collective-permute-done | bytes 73760 | tf_op jit(solution)/shard_map/ppermute | solution.py:207
  1.7 0.2 shard_map.74
  1.9 3.0 %collective-permute-start.1 = (bf16[144,128]{1,0:T(8,128)(2,1)S(1)}, bf16[144,128]{1,0:T(8,128)(2,1)S(1)}, u32[]{:S(2)}, u32[]{:S(2)}) collective-permute-start(bf16[144,128]{1,0:T(8,128)(2,1)S(1)} %shard_map.74), channel_id=1, source_target_pairs={{0,4},{4,0},{8,12},{12,8},{1,5},{5,1},{9,13},{13,9},{2,6},{6,2},{1... | collective-permute-start | bytes 110600 | tf_op jit(solution)/shard_map/ppermute | solution.py:207
  4.9 2.6 %collective-permute-start.2 = (bf16[144,128]{1,0:T(8,128)(2,1)S(1)}, bf16[144,128]{1,0:T(8,128)(2,1)S(1)}, u32[]{:S(2)}, u32[]{:S(2)}) collective-permute-start(bf16[144,128]{1,0:T(8,128)(2,1)S(1)} %shard_map.74), channel_id=1, source_target_pairs={{0,8},{4,12},{8,0},{12,4},{1,9},{5,13},{9,1},{13,5},{2,10},{6,14},... | collective-permute-start | bytes 110600 | tf_op jit(solution)/shard_map/ppermute | solution.py:207
  7.5 0.0 collective-permute-start.3
  7.5 0.0 collective-permute-done.1
  7.5 3.0 %collective-permute-done.2 = bf16[144,128]{1,0:T(8,128)(2,1)S(1)} collective-permute-done((bf16[144,128]{1,0:T(8,128)(2,1)S(1)}, bf16[144,128]{1,0:T(8,128)(2,1)S(1)}, u32[]{:S(2)}, u32[]{:S(2)}) %collective-permute-start.2) | collective-permute-done | bytes 36896 | tf_op jit(solution)/shard_map/ppermute | solution.py:207
  10.5 2.8 %collective-permute-done.3 = bf16[144,128]{1,0:T(8,128)(2,1)S(1)} collective-permute-done((bf16[144,128]{1,0:T(8,128)(2,1)S(1)}, bf16[144,128]{1,0:T(8,128)(2,1)S(1)}, u32[]{:S(2)}, u32[]{:S(2)}) %collective-permute-start.3) | collective-permute-done | bytes 36896 | tf_op jit(solution)/shard_map/ppermute | solution.py:207
  13.3 0.0 copy-start.3
  13.3 0.0 copy-start.4
  13.3 0.0 copy-start.5
  13.3 1.6 %collective-permute-start.4 = (bf16[4,144,128]{2,1,0:T(8,128)(2,1)S(1)}, bf16[4,144,128]{2,1,0:T(8,128)(2,1)S(1)}, u32[]{:S(2)}, u32[]{:S(2)}) collective-permute-start(bf16[4,144,128]{2,1,0:T(8,128)(2,1)S(1)} %pad_maximum_fusion.1.own), channel_id=1, source_target_pairs={{0,2},{2,0},{1,3},{3,1},{4,6},{6,4},{5,7},{7,5},{8,10},{10,8},{9,1... | collective-permute-start | bytes 442376 | tf_op jit(solution)/shard_map/ppermute | solution.py:207
  14.9 0.0 copy-done.3
  14.9 0.0 copy-done.4
  14.9 0.0 copy-done.5
  14.9 0.0 copy-start.6
  14.9 0.0 copy-start.7
  14.9 0.1 collective-permute-start.7
  15.0 0.5 %collective-permute-start.6 = (bf16[4,144,128]{2,1,0:T(8,128)(2,1)S(1)}, bf16[4,144,128]{2,1,0:T(8,128)(2,1)S(1)}, u32[]{:S(2)}, u32[]{:S(2)}) collective-permute-start(bf16[4,144,128]{2,1,0:T(8,128)(2,1)S(1)} %pad_maximum_fusion.1.own), channel_id=1, source_target_pairs={{0,1},{1,0},{2,3},{3,2},{4,5},{5,4},{6,7},{7,6},{8,9},{9,8},{10,11... | collective-permute-start | bytes 442376 | tf_op jit(solution)/shard_map/ppermute | solution.py:207
  15.5 3.0 %collective-permute-done.4.own = bf16[4,144,128]{2,1,0:T(8,128)(2,1)S(1)} collective-permute-done((bf16[4,144,128]{2,1,0:T(8,128)(2,1)S(1)}, bf16[4,144,128]{2,1,0:T(8,128)(2,1)S(1)}, u32[]{:S(2)}, u32[]{:S(2)}) %collective-permute-start.4) | collective-permute-done | bytes 147488 | tf_op jit(solution)/shard_map/ppermute | solution.py:207
  18.5 0.0 collective-permute-start.5
  18.5 0.0 copy-done.6
  18.5 0.0 copy-done.7
  18.6 0.0 copy-start.2
  18.6 0.6 %collective-permute-start.8 = (f32[4,64]{1,0:T(4,128)S(1)}, f32[4,64]{1,0:T(4,128)S(1)}, u32[]{:S(2)}, u32[]{:S(2)}) collective-permute-start(f32[4,64]{1,0:T(4,128)S(1)} %pad_maximum_fusion.2.own_gains), channel_id=1, source_target_pairs={{0,1},{1,0},{2,3},{3,2},{4,5},{5,4},{6,7},{7,6},{8,9},{9,8},{10,11... | collective-permute-start | bytes 3080 | tf_op jit(solution)/shard_map/ppermute | solution.py:207
  19.1 0.8 %collective-permute-done.8.other_gains = f32[4,64]{1,0:T(4,128)S(1)} collective-permute-done((f32[4,64]{1,0:T(4,128)S(1)}, f32[4,64]{1,0:T(4,128)S(1)}, u32[]{:S(2)}, u32[]{:S(2)}) %collective-permute-start.8) | collective-permute-done | bytes 1056 | tf_op jit(solution)/shard_map/ppermute | solution.py:207
  19.9 0.0 collective-permute-done.7.other
  20.0 0.0 copy-done.2
  20.0 0.4 %shard_map.75 = (bf16[2,128,256]{2,1,0:T(8,128)(2,1)S(1)}, bf16[2,128,256]{2,1,0:T(8,128)(2,1)S(1)}, bf16[2,128,128]{2,1,0:T(8,128)(2,1)S(1)}, bf16[2,128,128]{2...) custom-call(bf16[2,6,64,128]{3,2,1,0:T(8,128)(2,1)S(1)} %pad_maximum_fusion.own, ...), custom_call_target="tpu_custom_call" | custom-call | flops 1048576 | bytes 65536 | tf_op jit(solution)/shard_map/pallas_call | solution.py:211
  20.3 0.0 collective-permute-done.6.other
  20.3 0.7 %shard_map.76 = (f32[1160,128]{1,0:T(8,128)S(1)}, f32[1160,128]{1,0:T(8,128)S(1)}, f32[1152,128]{1,0:T(8,128)S(1)}, f32[960,128]{1,0:T(8,128)S(1)}) custom-call(bf16[4,144,128]{2,1,0:T(8,128)(2,1)S(1)} %pad_maximum_fusion.1.own, bf16[4,144,128]{2,1,0:T(8,128)(2,1)S(1)} %collective-permute-done.6.other, f32[56,128]{1,0:T(8,128)S(1)} %get-tuple-element.15.mask, ...), custom_call_target="tpu_custom_call" | custom-call | flops 67108864 | bytes 65536 | tf_op jit(solution)/shard_map/pallas_call | solution.py:211
  21.0 0.0 copy-start.1
  21.0 1.8 %shard_map.77.near_tri = f32[1920,128]{1,0:T(8,128)S(1)} custom-call(f32[1152,128]{1,0:T(8,128)S(1)} %get-tuple-element.21.left, f32[960,128]{1,0:T(8,128)S(1)} %get-tuple-element.22.rightt), custom_call_target="tpu_custom_call" | custom-call | flops 67108864 | bytes 65536 | tf_op jit(solution)/shard_map/pallas_call | solution.py:211
  22.9 0.0 collective-permute-done.5.other
  22.9 0.0 copy-done.1
  22.9 5.7 %shard_map.78 = f32[12,24,64]{2,1,0:T(8,128)} custom-call(bf16[4,144,128]{2,1,0:T(8,128)(2,1)S(1)} %collective-permute-done.4.own, bf16[4,144,128]{2,1,0:T(8,128)(2,1)S(1)} %collective-permute-done.5.other, f32[1160,128]{1,0:T(8,128)S(1)} %get-tuple-element.19.near_raw, f32[1160,128]{1,0:T(8,128)S(1)} %get-tuple-element.20.near_normed, ...), custom_call_target="tpu_custom_call" | custom-call | flops 1048576 | bytes 65536 | tf_op jit(solution)/shard_map/pallas_call | solution.py:211
  (4 shorter events, 0.1 us)
Async XLA Ops:
  0.0 1.7 %collective-permute-start = (f32[12,24,64]{2,1,0:T(8,128)}, f32[12,24,64]{2,1,0:T(8,128)S(1)}, u32[]{:S(2)}, u32[]{:S(2)}) collective-permute-start(f32[12,24,64]{2,1,0:T(8,128)} %bitcast.14), channel_id=1, source_target_pairs={{0,1},{1,0},{2,3},{3,2},{4,5},{5,4},{6,7},{7,6},{8,9},{9,8},{10,11... | collective-permute-start | bytes 221192 | tf_op jit(solution)/shard_map/ppermute | solution.py:207
  0.5 0.9 %copy-start = (f32[64,12,24]{0,2,1:T(8,128)S(1)}, f32[64,12,24]{0,2,1:T(8,128)}, u32[]{:S(2)}) copy-start(f32[64,12,24]{0,2,1:T(8,128)} %param.7) | copy-start | bytes 221188
  1.9 5.6 %collective-permute-start.1 = (bf16[144,128]{1,0:T(8,128)(2,1)S(1)}, bf16[144,128]{1,0:T(8,128)(2,1)S(1)}, u32[]{:S(2)}, u32[]{:S(2)}) collective-permute-start(bf16[144,128]{1,0:T(8,128)(2,1)S(1)} %shard_map.74), channel_id=1, source_target_pairs={{0,4},{4,0},{8,12},{12,8},{1,5},{5,1},{9,13},{13,9},{2,6},{6,2},{1... | collective-permute-start | bytes 110600 | tf_op jit(solution)/shard_map/ppermute | solution.py:207
  4.9 5.6 %collective-permute-start.2 = (bf16[144,128]{1,0:T(8,128)(2,1)S(1)}, bf16[144,128]{1,0:T(8,128)(2,1)S(1)}, u32[]{:S(2)}, u32[]{:S(2)}) collective-permute-start(bf16[144,128]{1,0:T(8,128)(2,1)S(1)} %shard_map.74), channel_id=1, source_target_pairs={{0,8},{4,12},{8,0},{12,4},{1,9},{5,13},{9,1},{13,5},{2,10},{6,14},... | collective-permute-start | bytes 110600 | tf_op jit(solution)/shard_map/ppermute | solution.py:207
  7.5 5.8 %collective-permute-start.3 = (bf16[144,128]{1,0:T(8,128)(2,1)S(1)}, bf16[144,128]{1,0:T(8,128)(2,1)S(1)}, u32[]{:S(2)}, u32[]{:S(2)}) collective-permute-start(bf16[144,128]{1,0:T(8,128)(2,1)S(1)} %shard_map.74), channel_id=1, source_target_pairs={{0,12},{4,8},{8,4},{12,0},{1,13},{5,9},{9,5},{13,1},{2,14},{6,10},... | collective-permute-start | bytes 110600 | tf_op jit(solution)/shard_map/ppermute | solution.py:207
  13.3 1.6 %copy-start.3 = (bf16[2,4,128,64]{2,3,1,0:T(8,128)(2,1)S(1)}, bf16[2,4,128,64]{2,3,1,0:T(8,128)(2,1)}, u32[]{:S(2)}) copy-start(bf16[2,4,128,64]{2,3,1,0:T(8,128)(2,1)} %param.10) | copy-start | bytes 393220
  13.3 1.6 %copy-start.4 = (bf16[2,128,64]{1,2,0:T(8,128)(2,1)S(1)}, bf16[2,128,64]{1,2,0:T(8,128)(2,1)}, u32[]{:S(2)}) copy-start(bf16[2,128,64]{1,2,0:T(8,128)(2,1)} %param.13) | copy-start | bytes 98308
  13.3 1.6 %copy-start.5 = (bf16[2,128,64]{1,2,0:T(8,128)(2,1)S(1)}, bf16[2,128,64]{1,2,0:T(8,128)(2,1)}, u32[]{:S(2)}) copy-start(bf16[2,128,64]{1,2,0:T(8,128)(2,1)} %param.11) | copy-start | bytes 98308
  13.3 5.2 %collective-permute-start.4 = (bf16[4,144,128]{2,1,0:T(8,128)(2,1)S(1)}, bf16[4,144,128]{2,1,0:T(8,128)(2,1)S(1)}, u32[]{:S(2)}, u32[]{:S(2)}) collective-permute-start(bf16[4,144,128]{2,1,0:T(8,128)(2,1)S(1)} %pad_maximum_fusion.1.own), channel_id=1, source_target_pairs={{0,2},{2,0},{1,3},{3,1},{4,6},{6,4},{5,7},{7,5},{8,10},{10,8},{9,1... | collective-permute-start | bytes 442376 | tf_op jit(solution)/shard_map/ppermute | solution.py:207
  14.9 3.6 %copy-start.6 = (f32[2,64]{1,0:T(2,128)S(1)}, f32[2,64]{1,0:T(2,128)}, u32[]{:S(2)}) copy-start(f32[2,64]{1,0:T(2,128)} %param.12) | copy-start | bytes 1540
  14.9 3.6 %copy-start.7 = (f32[2,64]{1,0:T(2,128)S(1)}, f32[2,64]{1,0:T(2,128)}, u32[]{:S(2)}) copy-start(f32[2,64]{1,0:T(2,128)} %param.9) | copy-start | bytes 1540
  14.9 5.0 %collective-permute-start.7 = (bf16[2,6,64,128]{3,2,1,0:T(8,128)(2,1)S(1)}, bf16[2,6,64,128]{3,2,1,0:T(8,128)(2,1)S(1)}, u32[]{:S(2)}, u32[]{:S(2)}) collective-permute-start(bf16[2,6,64,128]{3,2,1,0:T(8,128)(2,1)S(1)} %pad_maximum_fusion.own), channel_id=1, source_target_pairs={{0,1},{1,0},{2,3},{3,2},{4,5},{5,4},{6,7},{7,6},{8,9},{9,8},{10,11... | collective-permute-start | bytes 589832 | tf_op jit(solution)/shard_map/ppermute | solution.py:207
  15.0 5.3 %collective-permute-start.6 = (bf16[4,144,128]{2,1,0:T(8,128)(2,1)S(1)}, bf16[4,144,128]{2,1,0:T(8,128)(2,1)S(1)}, u32[]{:S(2)}, u32[]{:S(2)}) collective-permute-start(bf16[4,144,128]{2,1,0:T(8,128)(2,1)S(1)} %pad_maximum_fusion.1.own), channel_id=1, source_target_pairs={{0,1},{1,0},{2,3},{3,2},{4,5},{5,4},{6,7},{7,6},{8,9},{9,8},{10,11... | collective-permute-start | bytes 442376 | tf_op jit(solution)/shard_map/ppermute | solution.py:207
  18.5 4.3 %collective-permute-start.5 = (bf16[4,144,128]{2,1,0:T(8,128)(2,1)S(1)}, bf16[4,144,128]{2,1,0:T(8,128)(2,1)S(1)}, u32[]{:S(2)}, u32[]{:S(2)}) collective-permute-start(bf16[4,144,128]{2,1,0:T(8,128)(2,1)S(1)} %collective-permute-done.4.own), channel_id=1, source_target_pairs={{0,1},{1,0},{2,3},{3,2},{4,5},{5,4},{6,7},{7,6},{8,9},{9,8},{10,11... | collective-permute-start | bytes 442376 | tf_op jit(solution)/shard_map/ppermute | solution.py:207
  18.6 1.4 %copy-start.2 = (s32[48]{0:T(128)S(1)}, s32[48]{0:T(128)}, u32[]{:S(2)}) copy-start(s32[48]{0:T(128)} %param.8) | copy-start | bytes 580
  18.6 1.4 %collective-permute-start.8 = (f32[4,64]{1,0:T(4,128)S(1)}, f32[4,64]{1,0:T(4,128)S(1)}, u32[]{:S(2)}, u32[]{:S(2)}) collective-permute-start(f32[4,64]{1,0:T(4,128)S(1)} %pad_maximum_fusion.2.own_gains), channel_id=1, source_target_pairs={{0,1},{1,0},{2,3},{3,2},{4,5},{5,4},{6,7},{7,6},{8,9},{9,8},{10,11... | collective-permute-start | bytes 3080 | tf_op jit(solution)/shard_map/ppermute | solution.py:207
  21.0 1.8 %copy-start.1 = (f32[64,12,24]{0,2,1:T(8,128)S(1)}, f32[64,12,24]{0,2,1:T(8,128)}, u32[]{:S(2)}) copy-start(f32[64,12,24]{0,2,1:T(8,128)} %param.7) | copy-start | bytes 221188
where the time goes:
time: 28.7 us; the launch traced here: 28.6 us
  waiting for transfers between devices  9.89 us (34%)
  Pallas kernels  8.83 us (31%)
  starting transfers between devices  8.76 us (31%)
  local copies, waits for them, and re-layouts  0.94 us (3%)
    ppermute x9, waiting for transfers between devices, swap(): return lax.ppermute(x, axis, [(i, i ^ mask) for i in range(size)])  9.89 us
    pallas_call x6, Pallas kernels, call(): pl.pallas_call(kernel, out_shape=out_shape, scratch_shapes=list(scratch),...  8.83 us
    ppermute x9, starting transfers between devices, swap(): return lax.ppermute(x, axis, [(i, i ^ mask) for i in range(size)])  8.76 us
    unnamed x16, local copies, waits for them, and re-layouts  0.94 us
  transfers between devices with their start and end apart: 9, of which 5 were waited for; matrix products, arithmetic and copies ran while one was open for 0% of the time, Pallas kernels for 10%

commit v1 on v0

--- a/solution.py
+++ b/solution.py
@@ -33,10 +33,11 @@
     return pl.ds(first if isinstance(first, int) else pl.multiple_of(first, 8), count)
 
 
-def own_kernel(tile, out):
+def own_kernel(tile, out, whole):
     half = tile.shape[0] // 2
     rows = tile[pl.ds(lax.axis_index("gz") * half, half)]
     out[...] = rows.reshape(out.shape)
+    whole[...] = tile[...]
 
 
 def centre_kernel(own, other, out):
@@ -247,7 +248,9 @@
     other_weights = swap(own_weights, "gz")
     other_gains = swap(own_gains, "gz")
 
-    own_rows = call(own_kernel, jax.ShapeDtypeStruct((half * tile_cols, part), F32), tile)
+    own_rows, kept_tile = call(
+        own_kernel, [jax.ShapeDtypeStruct((half * tile_cols, part), F32), jax.ShapeDtypeStruct(tile.shape, F32)], tile
+    )
     message = call(centre_kernel, narrow(half * tile_cols, ch), own_rows, other_tile)
     column = [message]
     for s in range(1, blocks):
@@ -277,7 +280,7 @@
     result = call(
         functools.partial(far_kernel, place=place),
         jax.ShapeDtypeStruct(tile.shape, F32),
-        far, far_other, near_raw, near_normed, near_tri, mask, gains, wleft, wright, wgate, wout, tile,
+        far, far_other, near_raw, near_normed, near_tri, mask, gains, wleft, wright, wgate, wout, kept_tile,
         scratch=[
             vmem(pairs + 8),
             vmem(pairs + 8),

time: 28.7 us -> 28.7 us (level)
    unnamed x16 -> x14, local copies, waits for them, and re-layouts: 0.94 us -> 0.94 us
where the time goes in v1:
time: 28.7 us; the launch traced here: 28.6 us
  waiting for transfers between devices  9.88 us (34%)
  Pallas kernels  8.84 us (31%)
  starting transfers between devices  8.76 us (31%)
  local copies, waits for them, and re-layouts  0.94 us (3%)
    ppermute x9, waiting for transfers between devices, swap(): return lax.ppermute(x, axis, [(i, i ^ mask) for i in range(size)])  9.88 us
    pallas_call x6, Pallas kernels, call(): pl.pallas_call(kernel, out_shape=out_shape, scratch_shapes=list(scratch),...  8.84 us
    ppermute x9, starting transfers between devices, swap(): return lax.ppermute(x, axis, [(i, i ^ mask) for i in range(size)])  8.76 us
    unnamed x14, local copies, waits for them, and re-layouts  0.94 us
  transfers between devices with their start and end apart: 9, of which 5 were waited for; matrix products, arithmetic and copies ran while one was open for 0% of the time, Pallas kernels for 10%

profile of v1, /device:TPU:0, one launch (start us, length us, event | category | flops | bytes accessed | tf_op | source)
XLA Modules:
  0.0 28.6 jit_solution(17542381203657040815)
XLA Ops:
  0.0 0.5 %collective-permute-start = (f32[12,24,64]{2,1,0:T(8,128)}, f32[12,24,64]{2,1,0:T(8,128)S(1)}, u32[]{:S(2)}, u32[]{:S(2)}) collective-permute-start(f32[12,24,64]{2,1,0:T(8,128)} %bitcast.15), channel_id=1, source_target_pairs={{0,1},{1,0},{2,3},{3,2},{4,5},{5,4},{6,7},{7,6},{8,9},{9,8},{10,11... | collective-permute-start | bytes 221192 | tf_op jit(solution)/shard_map/ppermute | solution.py:208
  0.5 0.0 copy-start
  0.5 0.9 %copy-done = f32[64,12,24]{0,2,1:T(8,128)S(1)} copy-done((f32[64,12,24]{0,2,1:T(8,128)S(1)}, f32[64,12,24]{0,2,1:T(8,128)}, u32[]{:S(2)}) %copy-start) | copy-done | bytes 73752
  1.4 0.3 %collective-permute-done.other = f32[12,24,64]{2,1,0:T(8,128)S(1)} collective-permute-done((f32[12,24,64]{2,1,0:T(8,128)}, f32[12,24,64]{2,1,0:T(8,128)S(1)}, u32[]{:S(2)}, u32[]{:S(2)}) %collective-permute-start) | collective-permute-done | bytes 73760 | tf_op jit(solution)/shard_map/ppermute | solution.py:208
  1.7 0.2 shard_map.74
  1.9 3.0 %collective-permute-start.1 = (bf16[144,128]{1,0:T(8,128)(2,1)S(1)}, bf16[144,128]{1,0:T(8,128)(2,1)S(1)}, u32[]{:S(2)}, u32[]{:S(2)}) collective-permute-start(bf16[144,128]{1,0:T(8,128)(2,1)S(1)} %shard_map.74), channel_id=1, source_target_pairs={{0,4},{4,0},{8,12},{12,8},{1,5},{5,1},{9,13},{13,9},{2,6},{6,2},{1... | collective-permute-start | bytes 110600 | tf_op jit(solution)/shard_map/ppermute | solution.py:208
  4.9 2.6 %collective-permute-start.2 = (bf16[144,128]{1,0:T(8,128)(2,1)S(1)}, bf16[144,128]{1,0:T(8,128)(2,1)S(1)}, u32[]{:S(2)}, u32[]{:S(2)}) collective-permute-start(bf16[144,128]{1,0:T(8,128)(2,1)S(1)} %shard_map.74), channel_id=1, source_target_pairs={{0,8},{4,12},{8,0},{12,4},{1,9},{5,13},{9,1},{13,5},{2,10},{6,14},... | collective-permute-start | bytes 110600 | tf_op jit(solution)/shard_map/ppermute | solution.py:208
  7.5 0.0 collective-permute-start.3
  7.5 0.0 collective-permute-done.1
  7.5 3.0 %collective-permute-done.2 = bf16[144,128]{1,0:T(8,128)(2,1)S(1)} collective-permute-done((bf16[144,128]{1,0:T(8,128)(2,1)S(1)}, bf16[144,128]{1,0:T(8,128)(2,1)S(1)}, u32[]{:S(2)}, u32[]{:S(2)}) %collective-permute-start.2) | collective-permute-done | bytes 36896 | tf_op jit(solution)/shard_map/ppermute | solution.py:208
  10.5 2.8 %collective-permute-done.3 = bf16[144,128]{1,0:T(8,128)(2,1)S(1)} collective-permute-done((bf16[144,128]{1,0:T(8,128)(2,1)S(1)}, bf16[144,128]{1,0:T(8,128)(2,1)S(1)}, u32[]{:S(2)}, u32[]{:S(2)}) %collective-permute-start.3) | collective-permute-done | bytes 36896 | tf_op jit(solution)/shard_map/ppermute | solution.py:208
  13.3 0.0 copy-start.2
  13.3 0.0 copy-start.3
  13.3 0.0 copy-start.4
  13.3 1.6 %collective-permute-start.4 = (bf16[4,144,128]{2,1,0:T(8,128)(2,1)S(1)}, bf16[4,144,128]{2,1,0:T(8,128)(2,1)S(1)}, u32[]{:S(2)}, u32[]{:S(2)}) collective-permute-start(bf16[4,144,128]{2,1,0:T(8,128)(2,1)S(1)} %pad_maximum_fusion.1.own), channel_id=1, source_target_pairs={{0,2},{2,0},{1,3},{3,1},{4,6},{6,4},{5,7},{7,5},{8,10},{10,8},{9,1... | collective-permute-start | bytes 442376 | tf_op jit(solution)/shard_map/ppermute | solution.py:208
  14.9 0.0 copy-done.2
  14.9 0.0 copy-done.3
  14.9 0.0 copy-done.4
  14.9 0.0 copy-start.5
  14.9 0.0 copy-start.6
  14.9 0.1 collective-permute-start.7
  15.0 0.5 %collective-permute-start.6 = (bf16[4,144,128]{2,1,0:T(8,128)(2,1)S(1)}, bf16[4,144,128]{2,1,0:T(8,128)(2,1)S(1)}, u32[]{:S(2)}, u32[]{:S(2)}) collective-permute-start(bf16[4,144,128]{2,1,0:T(8,128)(2,1)S(1)} %pad_maximum_fusion.1.own), channel_id=1, source_target_pairs={{0,1},{1,0},{2,3},{3,2},{4,5},{5,4},{6,7},{7,6},{8,9},{9,8},{10,11... | collective-permute-start | bytes 442376 | tf_op jit(solution)/shard_map/ppermute | solution.py:208
  15.5 3.0 %collective-permute-done.4.own = bf16[4,144,128]{2,1,0:T(8,128)(2,1)S(1)} collective-permute-done((bf16[4,144,128]{2,1,0:T(8,128)(2,1)S(1)}, bf16[4,144,128]{2,1,0:T(8,128)(2,1)S(1)}, u32[]{:S(2)}, u32[]{:S(2)}) %collective-permute-start.4) | collective-permute-done | bytes 147488 | tf_op jit(solution)/shard_map/ppermute | solution.py:208
  18.5 0.0 collective-permute-start.5
  18.5 0.0 copy-done.5
  18.5 0.0 copy-done.6
  18.6 0.0 copy-start.1
  18.6 0.6 %collective-permute-start.8 = (f32[4,64]{1,0:T(4,128)S(1)}, f32[4,64]{1,0:T(4,128)S(1)}, u32[]{:S(2)}, u32[]{:S(2)}) collective-permute-start(f32[4,64]{1,0:T(4,128)S(1)} %pad_maximum_fusion.2.own_gains), channel_id=1, source_target_pairs={{0,1},{1,0},{2,3},{3,2},{4,5},{5,4},{6,7},{7,6},{8,9},{9,8},{10,11... | collective-permute-start | bytes 3080 | tf_op jit(solution)/shard_map/ppermute | solution.py:208
  19.1 0.8 %collective-permute-done.8.other_gains = f32[4,64]{1,0:T(4,128)S(1)} collective-permute-done((f32[4,64]{1,0:T(4,128)S(1)}, f32[4,64]{1,0:T(4,128)S(1)}, u32[]{:S(2)}, u32[]{:S(2)}) %collective-permute-start.8) | collective-permute-done | bytes 1056 | tf_op jit(solution)/shard_map/ppermute | solution.py:208
  19.9 0.0 collective-permute-done.7.other
  20.0 0.0 copy-done.1
  20.0 0.4 %shard_map.75 = (bf16[2,128,256]{2,1,0:T(8,128)(2,1)S(1)}, bf16[2,128,256]{2,1,0:T(8,128)(2,1)S(1)}, bf16[2,128,128]{2,1,0:T(8,128)(2,1)S(1)}, bf16[2,128,128]{2...) custom-call(bf16[2,6,64,128]{3,2,1,0:T(8,128)(2,1)S(1)} %pad_maximum_fusion.own, ...), custom_call_target="tpu_custom_call" | custom-call | flops 1048576 | bytes 65536 | tf_op jit(solution)/shard_map/pallas_call | solution.py:212
  20.3 0.0 collective-permute-done.6.other
  20.3 0.7 %shard_map.76 = (f32[1160,128]{1,0:T(8,128)S(1)}, f32[1160,128]{1,0:T(8,128)S(1)}, f32[1152,128]{1,0:T(8,128)S(1)}, f32[960,128]{1,0:T(8,128)S(1)}) custom-call(bf16[4,144,128]{2,1,0:T(8,128)(2,1)S(1)} %pad_maximum_fusion.1.own, bf16[4,144,128]{2,1,0:T(8,128)(2,1)S(1)} %collective-permute-done.6.other, f32[56,128]{1,0:T(8,128)S(1)} %get-tuple-element.18.mask, ...), custom_call_target="tpu_custom_call" | custom-call | flops 67108864 | bytes 65536 | tf_op jit(solution)/shard_map/pallas_call | solution.py:212
  21.0 1.8 %shard_map.77.near_tri = f32[1920,128]{1,0:T(8,128)S(1)} custom-call(f32[1152,128]{1,0:T(8,128)S(1)} %get-tuple-element.24.left, f32[960,128]{1,0:T(8,128)S(1)} %get-tuple-element.25.rightt), custom_call_target="tpu_custom_call" | custom-call | flops 67108864 | bytes 65536 | tf_op jit(solution)/shard_map/pallas_call | solution.py:212
  22.8 0.0 collective-permute-done.5.other
  22.9 5.7 %shard_map.78 = f32[12,24,64]{2,1,0:T(8,128)} custom-call(bf16[4,144,128]{2,1,0:T(8,128)(2,1)S(1)} %collective-permute-done.4.own, bf16[4,144,128]{2,1,0:T(8,128)(2,1)S(1)} %collective-permute-done.5.other, f32[1160,128]{1,0:T(8,128)S(1)} %get-tuple-element.22.near_raw, f32[1160,128]{1,0:T(8,128)S(1)} %get-tuple-element.23.near_normed, ...), custom_call_target="tpu_custom_call" | custom-call | flops 1048576 | bytes 65536 | tf_op jit(solution)/shard_map/pallas_call | solution.py:212
  (4 shorter events, 0.1 us)
Async XLA Ops:
  0.0 1.7 %collective-permute-start = (f32[12,24,64]{2,1,0:T(8,128)}, f32[12,24,64]{2,1,0:T(8,128)S(1)}, u32[]{:S(2)}, u32[]{:S(2)}) collective-permute-start(f32[12,24,64]{2,1,0:T(8,128)} %bitcast.15), channel_id=1, source_target_pairs={{0,1},{1,0},{2,3},{3,2},{4,5},{5,4},{6,7},{7,6},{8,9},{9,8},{10,11... | collective-permute-start | bytes 221192 | tf_op jit(solution)/shard_map/ppermute | solution.py:208
  0.5 0.9 %copy-start = (f32[64,12,24]{0,2,1:T(8,128)S(1)}, f32[64,12,24]{0,2,1:T(8,128)}, u32[]{:S(2)}) copy-start(f32[64,12,24]{0,2,1:T(8,128)} %param.7) | copy-start | bytes 221188
  1.9 5.6 %collective-permute-start.1 = (bf16[144,128]{1,0:T(8,128)(2,1)S(1)}, bf16[144,128]{1,0:T(8,128)(2,1)S(1)}, u32[]{:S(2)}, u32[]{:S(2)}) collective-permute-start(bf16[144,128]{1,0:T(8,128)(2,1)S(1)} %shard_map.74), channel_id=1, source_target_pairs={{0,4},{4,0},{8,12},{12,8},{1,5},{5,1},{9,13},{13,9},{2,6},{6,2},{1... | collective-permute-start | bytes 110600 | tf_op jit(solution)/shard_map/ppermute | solution.py:208
  4.9 5.6 %collective-permute-start.2 = (bf16[144,128]{1,0:T(8,128)(2,1)S(1)}, bf16[144,128]{1,0:T(8,128)(2,1)S(1)}, u32[]{:S(2)}, u32[]{:S(2)}) collective-permute-start(bf16[144,128]{1,0:T(8,128)(2,1)S(1)} %shard_map.74), channel_id=1, source_target_pairs={{0,8},{4,12},{8,0},{12,4},{1,9},{5,13},{9,1},{13,5},{2,10},{6,14},... | collective-permute-start | bytes 110600 | tf_op jit(solution)/shard_map/ppermute | solution.py:208
  7.5 5.8 %collective-permute-start.3 = (bf16[144,128]{1,0:T(8,128)(2,1)S(1)}, bf16[144,128]{1,0:T(8,128)(2,1)S(1)}, u32[]{:S(2)}, u32[]{:S(2)}) collective-permute-start(bf16[144,128]{1,0:T(8,128)(2,1)S(1)} %shard_map.74), channel_id=1, source_target_pairs={{0,12},{4,8},{8,4},{12,0},{1,13},{5,9},{9,5},{13,1},{2,14},{6,10},... | collective-permute-start | bytes 110600 | tf_op jit(solution)/shard_map/ppermute | solution.py:208
  13.3 1.6 %copy-start.2 = (bf16[2,4,128,64]{2,3,1,0:T(8,128)(2,1)S(1)}, bf16[2,4,128,64]{2,3,1,0:T(8,128)(2,1)}, u32[]{:S(2)}) copy-start(bf16[2,4,128,64]{2,3,1,0:T(8,128)(2,1)} %param.10) | copy-start | bytes 393220
  13.3 1.6 %copy-start.3 = (bf16[2,128,64]{1,2,0:T(8,128)(2,1)S(1)}, bf16[2,128,64]{1,2,0:T(8,128)(2,1)}, u32[]{:S(2)}) copy-start(bf16[2,128,64]{1,2,0:T(8,128)(2,1)} %param.13) | copy-start | bytes 98308
  13.3 1.6 %copy-start.4 = (bf16[2,128,64]{1,2,0:T(8,128)(2,1)S(1)}, bf16[2,128,64]{1,2,0:T(8,128)(2,1)}, u32[]{:S(2)}) copy-start(bf16[2,128,64]{1,2,0:T(8,128)(2,1)} %param.11) | copy-start | bytes 98308
  13.3 5.2 %collective-permute-start.4 = (bf16[4,144,128]{2,1,0:T(8,128)(2,1)S(1)}, bf16[4,144,128]{2,1,0:T(8,128)(2,1)S(1)}, u32[]{:S(2)}, u32[]{:S(2)}) collective-permute-start(bf16[4,144,128]{2,1,0:T(8,128)(2,1)S(1)} %pad_maximum_fusion.1.own), channel_id=1, source_target_pairs={{0,2},{2,0},{1,3},{3,1},{4,6},{6,4},{5,7},{7,5},{8,10},{10,8},{9,1... | collective-permute-start | bytes 442376 | tf_op jit(solution)/shard_map/ppermute | solution.py:208
  14.9 3.6 %copy-start.5 = (f32[2,64]{1,0:T(2,128)S(1)}, f32[2,64]{1,0:T(2,128)}, u32[]{:S(2)}) copy-start(f32[2,64]{1,0:T(2,128)} %param.12) | copy-start | bytes 1540
  14.9 3.6 %copy-start.6 = (f32[2,64]{1,0:T(2,128)S(1)}, f32[2,64]{1,0:T(2,128)}, u32[]{:S(2)}) copy-start(f32[2,64]{1,0:T(2,128)} %param.9) | copy-start | bytes 1540
  14.9 5.0 %collective-permute-start.7 = (bf16[2,6,64,128]{3,2,1,0:T(8,128)(2,1)S(1)}, bf16[2,6,64,128]{3,2,1,0:T(8,128)(2,1)S(1)}, u32[]{:S(2)}, u32[]{:S(2)}) collective-permute-start(bf16[2,6,64,128]{3,2,1,0:T(8,128)(2,1)S(1)} %pad_maximum_fusion.own), channel_id=1, source_target_pairs={{0,1},{1,0},{2,3},{3,2},{4,5},{5,4},{6,7},{7,6},{8,9},{9,8},{10,11... | collective-permute-start | bytes 589832 | tf_op jit(solution)/shard_map/ppermute | solution.py:208
  15.0 5.3 %collective-permute-start.6 = (bf16[4,144,128]{2,1,0:T(8,128)(2,1)S(1)}, bf16[4,144,128]{2,1,0:T(8,128)(2,1)S(1)}, u32[]{:S(2)}, u32[]{:S(2)}) collective-permute-start(bf16[4,144,128]{2,1,0:T(8,128)(2,1)S(1)} %pad_maximum_fusion.1.own), channel_id=1, source_target_pairs={{0,1},{1,0},{2,3},{3,2},{4,5},{5,4},{6,7},{7,6},{8,9},{9,8},{10,11... | collective-permute-start | bytes 442376 | tf_op jit(solution)/shard_map/ppermute | solution.py:208
  18.5 4.3 %collective-permute-start.5 = (bf16[4,144,128]{2,1,0:T(8,128)(2,1)S(1)}, bf16[4,144,128]{2,1,0:T(8,128)(2,1)S(1)}, u32[]{:S(2)}, u32[]{:S(2)}) collective-permute-start(bf16[4,144,128]{2,1,0:T(8,128)(2,1)S(1)} %collective-permute-done.4.own), channel_id=1, source_target_pairs={{0,1},{1,0},{2,3},{3,2},{4,5},{5,4},{6,7},{7,6},{8,9},{9,8},{10,11... | collective-permute-start | bytes 442376 | tf_op jit(solution)/shard_map/ppermute | solution.py:208
  18.6 1.4 %copy-start.1 = (s32[48]{0:T(128)S(1)}, s32[48]{0:T(128)}, u32[]{:S(2)}) copy-start(s32[48]{0:T(128)} %param.8) | copy-start | bytes 580
  18.6 1.4 %collective-permute-start.8 = (f32[4,64]{1,0:T(4,128)S(1)}, f32[4,64]{1,0:T(4,128)S(1)}, u32[]{:S(2)}, u32[]{:S(2)}) collective-permute-start(f32[4,64]{1,0:T(4,128)S(1)} %pad_maximum_fusion.2.own_gains), channel_id=1, source_target_pairs={{0,1},{1,0},{2,3},{3,2},{4,5},{5,4},{6,7},{7,6},{8,9},{9,8},{10,11... | collective-permute-start | bytes 3080 | tf_op jit(solution)/shard_map/ppermute | solution.py:208

commit v2 on v1

--- a/solution.py
+++ b/solution.py
@@ -78,83 +78,128 @@
     def __init__(self, res, tile_rows, tile_cols):
         self.res, self.rows, self.cols = res, tile_rows, tile_cols
         self.half = tile_rows // 2
+        self.blocks = res // tile_rows
+        self.per_column = tile_cols // tile_rows
         self.ipad = -(-tile_rows // 8) * 8
         self.span = tile_cols + self.ipad
+        self.part = self.blocks * self.half
         self.row_block = lax.axis_index("gx")
         self.col_block = lax.axis_index("gy")
         self.core = lax.axis_index("gz")
         self.first_row = self.row_block * tile_rows
         self.first_col = self.col_block * tile_cols
 
-
-def column_phase(at, own, other, mask, gains, wleft, wright, raw, normed, left, rightt, column):
+    def which(self, own):
+        return self.core if own else 1 - self.core
+
+    def mask_rows(self, mask, own):
+        return [
+            mask[pl.ds((self.row_block ^ s) * self.rows + self.which(own) * self.half + q, 1), :]
+            for s in range(self.blocks)
+            for q in range(self.half)
+        ]
+
+
+def columns_part(at, source, mask, gains, wleft, wright, raw, normed, left, right, column):
+    cols = at.cols
+    size = at.half * cols
     ch = mask.shape[1]
-    cols, span = at.cols, at.span
-    for s in range(own.shape[0]):
-        for source, which in ((own, at.core), (other, 1 - at.core)):
-            x = source[s].astype(F32)
-            var = jnp.mean(x * x, axis=-1, keepdims=True)
-            first = ((at.row_block ^ s) * at.rows + which * at.half) * cols
-            where = pl.ds(pl.multiple_of(first, 8), at.half * cols)
-            raw[where, :] = x
-            normed[where, :] = x * lax.rsqrt(var + EPSILON) * gains[0:1, :]
-    pairs = at.res * cols
+    zs = []
+    for s in range(at.blocks):
+        x = source[s].astype(F32)
+        var = jnp.mean(x * x, axis=-1, keepdims=True)
+        zs.append(x * lax.rsqrt(var + EPSILON) * gains[0:1, :])
+        raw[s * size : (s + 1) * size, :] = x
+        normed[s * size : (s + 1) * size, :] = zs[s]
+    pairs = at.part * cols
     raw[pairs:, :] = jnp.zeros((raw.shape[0] - pairs, ch), F32)
     normed[pairs:, :] = jnp.zeros((raw.shape[0] - pairs, ch), F32)
-
     kmask = mask[rows_at(column * cols, cols), :]
-    y = gated(normed[:pairs, :], wleft[0]).reshape(at.res, cols, ch) * kmask[None]
+    y = gated(jnp.concatenate(zs, axis=0), wleft[0]).reshape(at.part, cols, ch) * kmask[None]
     left[...] = y.reshape(pairs, ch)
-
+    wanted = []
+    for t in range(at.per_column):
+        s = at.row_block ^ (at.col_block * at.per_column + t)
+        wanted.append(normed[rows_at(s * size, size), :])
+    right[...] = gated(jnp.concatenate(wanted + zs[:1], axis=0), wright[0])
+
+
+def place_right(at, right_own, right_other, rightt):
+    cols, span = at.cols, at.span
     for k in range(at.ipad - at.rows):
-        rightt[pl.ds(cols + at.rows + k, cols, stride=span), :] = jnp.zeros((cols, ch), F32)
-    for slot in range(0, cols + at.rows, at.rows):
-        row = at.first_col + slot if slot < cols else at.first_row
-        y = gated(normed[rows_at(row * cols, at.rows * cols), :], wright[0])
-        for q in range(at.rows):
-            rightt[pl.ds(slot + q, cols, stride=span), :] = y[q * cols : (q + 1) * cols]
-
-
-def triangle_phase(at, left, rightt, tri, start):
+        rightt[pl.ds(cols + at.rows + k, cols, stride=span), :] = jnp.zeros((cols, rightt.shape[1]), F32)
+    for right, which in ((right_own, at.core), (right_other, 1 - at.core)):
+        for t in range(at.per_column + 1):
+            for q in range(at.half):
+                first = (t * at.half + q) * cols
+                slot = t * at.rows + which * at.half + q
+                rightt[pl.ds(slot, cols, stride=span), :] = right[first : first + cols, :]
+
+
+def triangle_phase(at, left_own, left_other, rightt, tri, start):
     cols, span = at.cols, at.span
-    ch = left.shape[1]
+    ch = rightt.shape[1]
     count = 4
-
-    def tri_block(n, carry):
-        first = n * count
-
-        def add(k, accs):
-            r = rightt[pl.ds(pl.multiple_of(k * span, 8), span), :]
-            return tuple(acc + left[pl.ds((first + q) * cols + k, 1), :] * r for q, acc in enumerate(accs))
-
-        where = [pl.ds(pl.multiple_of((first + q) * span, 8), span) for q in range(count)]
-        accs = tuple(jnp.zeros((span, ch), F32) if start is None else start[w, :] for w in where)
-        accs = lax.fori_loop(0, cols, add, accs, unroll=min(cols, 24))
-        for w, acc in zip(where, accs):
-            tri[w, :] = acc
-        return carry
-
-    lax.fori_loop(0, at.res // count, tri_block, 0)
-
-
-def near_kernel(own, other, mask, gains, wleft, wright, raw, normed, left, rightt, *, place):
+    for left, base in ((left_own, 0), (left_other, at.part)):
+
+        def tri_block(n, carry, left=left, base=base):
+            def add(k, accs):
+                r = rightt[pl.ds(pl.multiple_of(k * span, 8), span), :]
+                return tuple(
+                    acc + left[pl.ds((n * count + q) * cols + k, 1), :] * r for q, acc in enumerate(accs)
+                )
+
+            where = [pl.ds(pl.multiple_of((base + n * count + q) * span, 8), span) for q in range(count)]
+            accs = tuple(jnp.zeros((span, ch), F32) if start is None else start[w, :] for w in where)
+            accs = lax.fori_loop(0, cols, add, accs, unroll=min(cols, 24))
+            for w, acc in zip(where, accs):
+                tri[w, :] = acc
+            return carry
+
+        lax.fori_loop(0, at.part // count, tri_block, 0)
+
+
+def near_own_kernel(source, mask, gains, wleft, wright, raw, normed, left, right, *, place):
     at = Place(*place)
-    column_phase(at, own, other, mask, gains, wleft, wright, raw, normed, left, rightt, at.col_block)
-
-
-def near_triangle_kernel(left, rightt, tri, *, place):
-    triangle_phase(Place(*place), left, rightt, tri, None)
-
-
-def far_kernel(
-    own, other, near_raw, near_normed, near_tri, mask, gains, wleft, wright, wgate, wout, pair, out,
-    raw, normed, left, rightt, tri, first_update, znext, right1, left1, *, place,
+    columns_part(at, source, mask, gains, wleft, wright, raw, normed, left, right, at.col_block)
+
+
+def near_other_kernel(
+    source, right_own, mask, gains, wleft, wright, raw, normed, left, rightt, right, *, place
 ):
     at = Place(*place)
-    res, rows, cols, ipad, span = at.res, at.rows, at.cols, at.ipad, at.span
+    columns_part(at, source, mask, gains, wleft, wright, raw, normed, left, right, at.col_block)
+    place_right(at, right_own, right, rightt)
+
+
+def near_triangle_kernel(left_own, left_other, rightt, tri, *, place):
+    triangle_phase(Place(*place), left_own, left_other, rightt, tri, None)
+
+
+def far_own_kernel(
+    source, near_own, near_other, mask, gains, wleft, wright, wgate, raw, normed, left, right, gate, *, place
+):
+    at = Place(*place)
+    columns_part(at, source, mask, gains, wleft, wright, raw, normed, left, right, 1 - at.col_block)
+    pairs = at.part * at.cols
+    for n, normed_near in enumerate((near_own, near_other)):
+        gate[n * pairs : (n + 1) * pairs, :] = jnp.tanh(dot(normed_near[:pairs, :], wgate[0])) + 1.0
+
+
+def far_kernel(
+    source, near_raws_own, near_raws_other, near_normed_own, near_normed_other, near_tri,
+    raw_own, normed_own, left_own, right_own, near_gate,
+    mask, gains, wleft, wright, wgate, wout, pair, out,
+    raw_other, normed_other, left_other, right_other, rightt, tri, first_update, znext, right1, left1, *, place,
+):
+    at = Place(*place)
+    res, rows, cols, ipad, span, half = at.res, at.rows, at.cols, at.ipad, at.span, at.half
     ch = mask.shape[1]
-    column_phase(at, own, other, mask, gains, wleft, wright, raw, normed, left, rightt, 1 - at.col_block)
-    triangle_phase(at, left, rightt, tri, near_tri)
+    columns_part(
+        at, source, mask, gains, wleft, wright, raw_other, normed_other, left_other, right_other, 1 - at.col_block
+    )
+    place_right(at, right_own, right_other, rightt)
+    triangle_phase(at, left_own, left_other, rightt, tri, near_tri)
     ones = jnp.full((ch, ch), 1.0 / ch, BF16)
     gain_in, gain_out = gains[0:2, :], gains[2:4, :]
 
@@ -163,25 +208,32 @@
     )
     row_is_near = at.first_row // cols == at.col_block
     offset = at.first_row % cols
-    zs, ns, ms = [], [], []
+    mrows = at.mask_rows(mask, True) + at.mask_rows(mask, False)
+    zs, ns = [], []
+    for near_raw, raw, near_normed, normed in (
+        (near_raws_own, raw_own, near_normed_own, normed_own),
+        (near_raws_other, raw_other, near_normed_other, normed_other),
+    ):
+        for r in range(at.part):
+            where = pl.ds(r * cols + offset, ipad)
+            zs += [near_raw[r * cols : (r + 1) * cols, :], jnp.where(row_is_near, near_raw[where, :], raw[where, :])]
+            ns.append(jnp.where(row_is_near, near_normed[where, :], normed[where, :]))
+    gate_rows = jnp.tanh(dot(jnp.concatenate(ns, axis=0), wgate[0])) + 1.0
+    gates = []
     for r in range(res):
-        where = pl.ds(r * cols + offset, ipad)
-        zs += [near_raw[r * cols : (r + 1) * cols, :], jnp.where(row_is_near, near_raw[where, :], raw[where, :])]
-        ns += [
-            near_normed[r * cols : (r + 1) * cols, :],
-            jnp.where(row_is_near, near_normed[where, :], normed[where, :]),
-        ]
-        ms.append(smask * mask[r : r + 1, :])
-    gate = jnp.tanh(dot(jnp.concatenate(ns, axis=0), wgate[0])) + 1.0
+        m = smask * mrows[r]
+        gates.append(near_gate[r * cols : (r + 1) * cols, :] * m[:cols])
+        gates.append(gate_rows[r * ipad : (r + 1) * ipad] * m[cols:])
     tn = lane_norm(tri[...], gain_out[0:1], ones)
-    update = gate * dot(tn, wout[0]) * jnp.concatenate(ms, axis=0)
+    update = jnp.concatenate(gates, axis=0) * dot(tn, wout[0])
     first_update[...] = update
     znext[...] = lane_norm(jnp.concatenate(zs, axis=0) + update, gain_in[1:2], ones)
 
     z3 = znext[...].reshape(res, span, ch)
     right1[...] = gated(z3[:, :cols].reshape(res * cols, ch), wright[1])
-    v = gated(z3[:, cols:].reshape(res * ipad, ch), wleft[1]).reshape(res, ipad, ch) * mask[:res, :][:, None, :]
-    left1[...] = v.reshape(res * ipad, ch)
+    v = gated(z3[:, cols:].reshape(res * ipad, ch), wleft[1])
+    for r in range(res):
+        left1[r * ipad : (r + 1) * ipad, :] = v[r * ipad : (r + 1) * ipad] * mrows[r]
 
     def tri1_block(k, accs):
         r = right1[pl.ds(pl.multiple_of(k * cols, 8), cols), :]
@@ -191,16 +243,16 @@
     tn = lane_norm(jnp.concatenate(accs, axis=0), gain_out[1:2], ones)
     ns, us, ms = [], [], []
     for i in range(rows):
-        where = pl.ds(pl.multiple_of((at.first_row + i) * span, 8), cols)
+        local = (at.core ^ (i // half)) * at.part + i % half
+        where = pl.ds(pl.multiple_of(local * span, 8), cols)
         ns.append(znext[where, :])
         us.append(first_update[where, :])
         ms.append(smask[:cols] * mask[pl.ds(at.first_row + i, 1), :])
-    gate = jnp.tanh(dot(jnp.concatenate(ns, axis=0), wgate[1])) + 1.0
-    update = gate * dot(tn, wout[1]) * jnp.concatenate(ms, axis=0)
-    moved = jnp.concatenate(us, axis=0) + update
+    gate = (jnp.tanh(dot(jnp.concatenate(ns, axis=0), wgate[1])) + 1.0) * jnp.concatenate(ms, axis=0)
     part = ch // 2
-    moved = pltpu.roll(moved, at.core * part, 1)[:, :part]
-    out[...] = pair[...] + moved.reshape(rows, cols, part)
+    before = pltpu.roll(jnp.concatenate(us, axis=0), at.core * part, 1)
+    moved = before + pltpu.roll(gate * dot(tn, wout[1]), at.core * part, 1)
+    out[...] = pair[...] + moved[:, :part].reshape(rows, cols, part)
 
 
 def swap(x, axis, mask=1):
@@ -265,26 +317,45 @@
     far = swap(near, "gy")
     near_other = swap(near, "gz")
     far_other = swap(far, "gz")
-    near_raw, near_normed, near_left, near_right = call(
-        functools.partial(near_kernel, place=place),
-        [wide(pairs + 8), wide(pairs + 8), wide(pairs), wide(tile_cols * span)],
-        near, near_other, mask, gains, wleft, wright,
-        flops=2**26,
+    part_pairs = pairs // 2
+    right_rows = (tile_cols + tile_rows) // 2 * tile_cols
+    part_shapes = [wide(part_pairs + 8), wide(part_pairs + 8), wide(part_pairs), wide(right_rows)]
+    parameters = (mask, gains, wleft, wright)
+    raw_own, normed_own, left_own, right_own = call(
+        functools.partial(near_own_kernel, place=place),
+        part_shapes,
+        near, *parameters,
+        flops=2**24,
+    )
+    raw_other, normed_other, left_other, near_right = call(
+        functools.partial(near_other_kernel, place=place),
+        part_shapes[:3] + [wide(tile_cols * span)],
+        near_other, right_own, *parameters,
+        scratch=[vmem(right_rows)],
+        flops=2**24,
     )
     near_tri = call(
         functools.partial(near_triangle_kernel, place=place),
         wide(res * span),
-        near_left, near_right,
+        left_own, left_other, near_right,
         flops=2**26,
+    )
+    *far_parts, near_gate = call(
+        functools.partial(far_own_kernel, place=place),
+        part_shapes + [wide(pairs)],
+        far, normed_own, normed_other, *parameters, wgate,
+        flops=2**24,
     )
     result = call(
         functools.partial(far_kernel, place=place),
         jax.ShapeDtypeStruct(tile.shape, F32),
-        far, far_other, near_raw, near_normed, near_tri, mask, gains, wleft, wright, wgate, wout, kept_tile,
+        far_other, raw_own, raw_other, normed_own, normed_other, near_tri, *far_parts, near_gate,
+        *parameters, wgate, wout, kept_tile,
         scratch=[
-            vmem(pairs + 8),
-            vmem(pairs + 8),
-            vmem(pairs),
+            vmem(part_pairs + 8),
+            vmem(part_pairs + 8),
+            vmem(part_pairs),
+            vmem(right_rows),
             vmem(tile_cols * span),
             vmem(res * span),
             vmem(res * span),
@@ -292,7 +363,7 @@
             vmem(pairs),
             vmem(res * ipad),
         ],
-        vmem_mib=24,
+        vmem_mib=20,
     )
     return jnp.transpose(result, (2, 0, 1))
 
@@ -379,7 +450,8 @@
         and res * res * part * 2 * 4 <= REPLICATED_LIMIT
         and lax.axis_size("gy") == 2
         and lax.axis_size("gx").bit_count() == 1
-        and res % 4 == 0
+        and res % 8 == 0
+        and res // tile_rows * (tile_rows // 2) % 4 == 0
         and tile_rows % 2 == 0
         and tile_cols % 8 == 0
         and tile_cols % tile_rows == 0

time: 28.7 us -> 27.7 us (0.965)
  waiting for transfers between devices: 9.88 us -> 8.35 us
  Pallas kernels: 8.84 us -> 9.24 us
    ppermute x9, waiting for transfers between devices: 9.88 us -> 8.35 us  [swap(): return lax.ppermute(x, axis, [(i, i ^ mask) for i in range(size)])]
    pallas_call x6 -> x8, Pallas kernels: 8.84 us -> 9.24 us  [call(): pl.pallas_call(kernel, out_shape=out_shape, scratch_shapes=list(scratch),...]
  transfers between devices with their start and end apart: 9 -> 9, of which waited for: 5 -> 5; matrix products, arithmetic and copies ran while one was open for 0% -> 0% of each run, Pallas kernels for 10% -> 14%
where the time goes in v2:
time: 27.7 us; the launch traced here: 27.6 us
  Pallas kernels  9.24 us (33%)
  starting transfers between devices  8.84 us (32%)
  waiting for transfers between devices  8.35 us (30%)
  local copies, waits for them, and re-layouts  0.94 us (3%)
    pallas_call x8, Pallas kernels, call(): pl.pallas_call(kernel, out_shape=out_shape, scratch_shapes=list(scratch),...  9.24 us
    ppermute x9, starting transfers between devices, swap(): return lax.ppermute(x, axis, [(i, i ^ mask) for i in range(size)])  8.84 us
    ppermute x9, waiting for transfers between devices, swap(): return lax.ppermute(x, axis, [(i, i ^ mask) for i in range(size)])  8.35 us
    unnamed x14, local copies, waits for them, and re-layouts  0.94 us
  transfers between devices with their start and end apart: 9, of which 5 were waited for; matrix products, arithmetic and copies ran while one was open for 0% of the time, Pallas kernels for 14%

profile of v2, /device:TPU:0, one launch (start us, length us, event | category | flops | bytes accessed | tf_op | source)
XLA Modules:
  0.0 27.6 jit_solution(16736813872112888051)
XLA Ops:
  0.0 0.5 %collective-permute-start = (f32[12,24,64]{2,1,0:T(8,128)}, f32[12,24,64]{2,1,0:T(8,128)S(1)}, u32[]{:S(2)}, u32[]{:S(2)}) collective-permute-start(f32[12,24,64]{2,1,0:T(8,128)} %bitcast.15), channel_id=1, source_target_pairs={{0,1},{1,0},{2,3},{3,2},{4,5},{5,4},{6,7},{7,6},{8,9},{9,8},{10,11... | collective-permute-start | bytes 221192 | tf_op jit(solution)/shard_map/ppermute | solution.py:260
  0.5 0.0 copy-start
  0.5 0.9 %copy-done = f32[64,12,24]{0,2,1:T(8,128)S(1)} copy-done((f32[64,12,24]{0,2,1:T(8,128)S(1)}, f32[64,12,24]{0,2,1:T(8,128)}, u32[]{:S(2)}) %copy-start) | copy-done | bytes 73752
  1.4 0.3 %collective-permute-done.other = f32[12,24,64]{2,1,0:T(8,128)S(1)} collective-permute-done((f32[12,24,64]{2,1,0:T(8,128)}, f32[12,24,64]{2,1,0:T(8,128)S(1)}, u32[]{:S(2)}, u32[]{:S(2)}) %collective-permute-start) | collective-permute-done | bytes 73760 | tf_op jit(solution)/shard_map/ppermute | solution.py:260
  1.7 0.2 shard_map.74
  1.9 5.0 %collective-permute-start.3 = (bf16[144,128]{1,0:T(8,128)(2,1)S(1)}, bf16[144,128]{1,0:T(8,128)(2,1)S(1)}, u32[]{:S(2)}, u32[]{:S(2)}) collective-permute-start(bf16[144,128]{1,0:T(8,128)(2,1)S(1)} %shard_map.74), channel_id=1, source_target_pairs={{0,12},{4,8},{8,4},{12,0},{1,13},{5,9},{9,5},{13,1},{2,14},{6,10},... | collective-permute-start | bytes 110600 | tf_op jit(solution)/shard_map/ppermute | solution.py:260
  7.0 0.0 collective-permute-start.2
  7.0 0.6 %collective-permute-start.1 = (bf16[144,128]{1,0:T(8,128)(2,1)S(1)}, bf16[144,128]{1,0:T(8,128)(2,1)S(1)}, u32[]{:S(2)}, u32[]{:S(2)}) collective-permute-start(bf16[144,128]{1,0:T(8,128)(2,1)S(1)} %shard_map.74), channel_id=1, source_target_pairs={{0,4},{4,0},{8,12},{12,8},{1,5},{5,1},{9,13},{13,9},{2,6},{6,2},{1... | collective-permute-start | bytes 110600 | tf_op jit(solution)/shard_map/ppermute | solution.py:260
  7.6 1.3 %collective-permute-done.3 = bf16[144,128]{1,0:T(8,128)(2,1)S(1)} collective-permute-done((bf16[144,128]{1,0:T(8,128)(2,1)S(1)}, bf16[144,128]{1,0:T(8,128)(2,1)S(1)}, u32[]{:S(2)}, u32[]{:S(2)}) %collective-permute-start.3) | collective-permute-done | bytes 36896 | tf_op jit(solution)/shard_map/ppermute | solution.py:260
  8.9 2.9 %collective-permute-done.2 = bf16[144,128]{1,0:T(8,128)(2,1)S(1)} collective-permute-done((bf16[144,128]{1,0:T(8,128)(2,1)S(1)}, bf16[144,128]{1,0:T(8,128)(2,1)S(1)}, u32[]{:S(2)}, u32[]{:S(2)}) %collective-permute-start.2) | collective-permute-done | bytes 36896 | tf_op jit(solution)/shard_map/ppermute | solution.py:260
  11.8 0.0 collective-permute-done.1
  11.8 0.0 copy-start.2
  11.8 0.0 copy-start.3
  11.8 0.0 copy-start.4
  11.9 1.6 %collective-permute-start.4 = (bf16[4,144,128]{2,1,0:T(8,128)(2,1)S(1)}, bf16[4,144,128]{2,1,0:T(8,128)(2,1)S(1)}, u32[]{:S(2)}, u32[]{:S(2)}) collective-permute-start(bf16[4,144,128]{2,1,0:T(8,128)(2,1)S(1)} %pad_maximum_fusion.1.source), channel_id=1, source_target_pairs={{0,2},{2,0},{1,3},{3,1},{4,6},{6,4},{5,7},{7,5},{8,10},{10,8},{9,1... | collective-permute-start | bytes 442376 | tf_op jit(solution)/shard_map/ppermute | solution.py:260
  13.4 0.0 copy-done.2
  13.4 0.0 copy-done.3
  13.4 0.0 copy-done.4
  13.4 0.0 copy-start.5
  13.4 0.0 copy-start.6
  13.5 0.1 collective-permute-start.6
  13.6 0.5 %collective-permute-start.8 = (bf16[4,144,128]{2,1,0:T(8,128)(2,1)S(1)}, bf16[4,144,128]{2,1,0:T(8,128)(2,1)S(1)}, u32[]{:S(2)}, u32[]{:S(2)}) collective-permute-start(bf16[4,144,128]{2,1,0:T(8,128)(2,1)S(1)} %pad_maximum_fusion.1.source), channel_id=1, source_target_pairs={{0,1},{1,0},{2,3},{3,2},{4,5},{5,4},{6,7},{7,6},{8,9},{9,8},{10,11... | collective-permute-start | bytes 442376 | tf_op jit(solution)/shard_map/ppermute | solution.py:260
  14.1 3.0 %collective-permute-done.4.source = bf16[4,144,128]{2,1,0:T(8,128)(2,1)S(1)} collective-permute-done((bf16[4,144,128]{2,1,0:T(8,128)(2,1)S(1)}, bf16[4,144,128]{2,1,0:T(8,128)(2,1)S(1)}, u32[]{:S(2)}, u32[]{:S(2)}) %collective-permute-start.4) | collective-permute-done | bytes 147488 | tf_op jit(solution)/shard_map/ppermute | solution.py:260
  17.1 0.0 collective-permute-start.5
  17.1 0.0 copy-done.5
  17.1 0.0 copy-done.6
  17.1 0.0 copy-start.1
  17.1 0.6 %collective-permute-start.7 = (f32[4,64]{1,0:T(4,128)S(1)}, f32[4,64]{1,0:T(4,128)S(1)}, u32[]{:S(2)}, u32[]{:S(2)}) collective-permute-start(f32[4,64]{1,0:T(4,128)S(1)} %pad_maximum_fusion.2.own_gains), channel_id=1, source_target_pairs={{0,1},{1,0},{2,3},{3,2},{4,5},{5,4},{6,7},{7,6},{8,9},{9,8},{10,11... | collective-permute-start | bytes 3080 | tf_op jit(solution)/shard_map/ppermute | solution.py:260
  17.7 0.8 %collective-permute-done.7.other_gains = f32[4,64]{1,0:T(4,128)S(1)} collective-permute-done((f32[4,64]{1,0:T(4,128)S(1)}, f32[4,64]{1,0:T(4,128)S(1)}, u32[]{:S(2)}, u32[]{:S(2)}) %collective-permute-start.7) | collective-permute-done | bytes 1056 | tf_op jit(solution)/shard_map/ppermute | solution.py:260
  18.5 0.0 collective-permute-done.6.other
  18.5 0.0 copy-done.1
  18.5 0.4 %shard_map.75 = (bf16[2,128,256]{2,1,0:T(8,128)(2,1)S(1)}, bf16[2,128,256]{2,1,0:T(8,128)(2,1)S(1)}, bf16[2,128,128]{2,1,0:T(8,128)(2,1)S(1)}, bf16[2,128,128]{2...) custom-call(bf16[2,6,64,128]{3,2,1,0:T(8,128)(2,1)S(1)} %pad_maximum_fusion.own, ...), custom_call_target="tpu_custom_call" | custom-call | flops 1048576 | bytes 65536 | tf_op jit(solution)/shard_map/pallas_call | solution.py:264
  18.9 0.4 %shard_map.76 = (f32[584,128]{1,0:T(8,128)S(1)}, f32[584,128]{1,0:T(8,128)S(1)}, f32[576,128]{1,0:T(8,128)S(1)}, f32[432,128]{1,0:T(8,128)S(1)}) custom-call(bf16[4,144,128]{2,1,0:T(8,128)(2,1)S(1)} %pad_maximum_fusion.1.source, f32[56,128]{1,0:T(8,128)S(1)} %get-tuple-element.27.mask, f32[4,128]{1,0:T(4,128)S(1)} %get-tuple-element.28.gains, ...), custom_call_target="tpu_custom_call" | custom-call | flops 16777216 | bytes 65536 | tf_op jit(solution)/shard_map/pallas_call | solution.py:264
  19.3 0.0 collective-permute-done.8.source
  19.3 0.4 %shard_map.77 = (f32[584,128]{1,0:T(8,128)S(1)}, f32[584,128]{1,0:T(8,128)S(1)}, f32[576,128]{1,0:T(8,128)S(1)}, f32[960,128]{1,0:T(8,128)S(1)}) custom-call(bf16[4,144,128]{2,1,0:T(8,128)(2,1)S(1)} %collective-permute-done.8.source, f32[432,128]{1,0:T(8,128)S(1)} %get-tuple-element.32.right_own, f32[56,128]{1,0:T(8,128)S(1)} %get-tuple-element.27.mask, ...), custom_call_target="tpu_custom_call" | custom-call | flops 16777216 | bytes 65536 | tf_op jit(solution)/shard_map/pallas_call | solution.py:264
  19.7 0.5 %shard_map.79 = (f32[584,128]{1,0:T(8,128)S(1)}, f32[584,128]{1,0:T(8,128)S(1)}, f32[576,128]{1,0:T(8,128)S(1)}, f32[432,128]{1,0:T(8,128)S(1)}, f32[1152,128]{1,0:T(8,128)S(1)}) custom-call(bf16[4,144,128]{2,1,0:T(8,128)(2,1)S(1)} %collective-permute-done.4.source, f32[584,128]{1,0:T(8,128)S(1)} %get-tuple-element.34.near_own.near_normed_own, ...), custom_call_target="tpu_custom_call" | custom-call | flops 16777216 | bytes 65536 | tf_op jit(solution)/shard_map/pallas_call | solution.py:264
  20.2 2.0 %shard_map.78.near_tri = f32[1920,128]{1,0:T(8,128)S(1)} custom-call(f32[576,128]{1,0:T(8,128)S(1)} %get-tuple-element.36.left_own, f32[576,128]{1,0:T(8,128)S(1)} %get-tuple-element.37.left_other, f32[960,128]{1,0:T(8,128)S(1)} %get-tuple-element.38.rightt), custom_call_target="tpu_custom_call" | custom-call | flops 67108864 | bytes 65536 | tf_op jit(solution)/shard_map/pallas_call | solution.py:264
  22.3 0.0 collective-permute-done.5.source
  22.3 5.3 %shard_map.80 = f32[12,24,64]{2,1,0:T(8,128)} custom-call(bf16[4,144,128]{2,1,0:T(8,128)(2,1)S(1)} %collective-permute-done.5.source, f32[584,128]{1,0:T(8,128)S(1)} %get-tuple-element.31.near_raws_own, f32[584,128]{1,0:T(8,128)S(1)} %get-tuple-element.33.near_raws_other, f32[584,128]{1,0:T(8,128)S(1)} %get-tuple-element.34.near_own.near_normed_own, ...), custom_call_target="tpu_custom_call" | custom-call | flops 1048576 | bytes 65536 | tf_op jit(solution)/shard_map/pallas_call | solution.py:264
  (4 shorter events, 0.1 us)
Async XLA Ops:
  0.0 1.7 %collective-permute-start = (f32[12,24,64]{2,1,0:T(8,128)}, f32[12,24,64]{2,1,0:T(8,128)S(1)}, u32[]{:S(2)}, u32[]{:S(2)}) collective-permute-start(f32[12,24,64]{2,1,0:T(8,128)} %bitcast.15), channel_id=1, source_target_pairs={{0,1},{1,0},{2,3},{3,2},{4,5},{5,4},{6,7},{7,6},{8,9},{9,8},{10,11... | collective-permute-start | bytes 221192 | tf_op jit(solution)/shard_map/ppermute | solution.py:260
  0.5 0.9 %copy-start = (f32[64,12,24]{0,2,1:T(8,128)S(1)}, f32[64,12,24]{0,2,1:T(8,128)}, u32[]{:S(2)}) copy-start(f32[64,12,24]{0,2,1:T(8,128)} %param.7) | copy-start | bytes 221188
  1.9 7.0 %collective-permute-start.3 = (bf16[144,128]{1,0:T(8,128)(2,1)S(1)}, bf16[144,128]{1,0:T(8,128)(2,1)S(1)}, u32[]{:S(2)}, u32[]{:S(2)}) collective-permute-start(bf16[144,128]{1,0:T(8,128)(2,1)S(1)} %shard_map.74), channel_id=1, source_target_pairs={{0,12},{4,8},{8,4},{12,0},{1,13},{5,9},{9,5},{13,1},{2,14},{6,10},... | collective-permute-start | bytes 110600 | tf_op jit(solution)/shard_map/ppermute | solution.py:260
  7.0 4.9 %collective-permute-start.2 = (bf16[144,128]{1,0:T(8,128)(2,1)S(1)}, bf16[144,128]{1,0:T(8,128)(2,1)S(1)}, u32[]{:S(2)}, u32[]{:S(2)}) collective-permute-start(bf16[144,128]{1,0:T(8,128)(2,1)S(1)} %shard_map.74), channel_id=1, source_target_pairs={{0,8},{4,12},{8,0},{12,4},{1,9},{5,13},{9,1},{13,5},{2,10},{6,14},... | collective-permute-start | bytes 110600 | tf_op jit(solution)/shard_map/ppermute | solution.py:260
  7.0 4.9 %collective-permute-start.1 = (bf16[144,128]{1,0:T(8,128)(2,1)S(1)}, bf16[144,128]{1,0:T(8,128)(2,1)S(1)}, u32[]{:S(2)}, u32[]{:S(2)}) collective-permute-start(bf16[144,128]{1,0:T(8,128)(2,1)S(1)} %shard_map.74), channel_id=1, source_target_pairs={{0,4},{4,0},{8,12},{12,8},{1,5},{5,1},{9,13},{13,9},{2,6},{6,2},{1... | collective-permute-start | bytes 110600 | tf_op jit(solution)/shard_map/ppermute | solution.py:260
  11.8 1.6 %copy-start.2 = (bf16[2,4,128,64]{2,3,1,0:T(8,128)(2,1)S(1)}, bf16[2,4,128,64]{2,3,1,0:T(8,128)(2,1)}, u32[]{:S(2)}) copy-start(bf16[2,4,128,64]{2,3,1,0:T(8,128)(2,1)} %param.10) | copy-start | bytes 393220
  11.8 1.6 %copy-start.3 = (bf16[2,128,64]{1,2,0:T(8,128)(2,1)S(1)}, bf16[2,128,64]{1,2,0:T(8,128)(2,1)}, u32[]{:S(2)}) copy-start(bf16[2,128,64]{1,2,0:T(8,128)(2,1)} %param.13) | copy-start | bytes 98308
  11.8 1.6 %copy-start.4 = (bf16[2,128,64]{1,2,0:T(8,128)(2,1)S(1)}, bf16[2,128,64]{1,2,0:T(8,128)(2,1)}, u32[]{:S(2)}) copy-start(bf16[2,128,64]{1,2,0:T(8,128)(2,1)} %param.11) | copy-start | bytes 98308
  11.9 5.2 %collective-permute-start.4 = (bf16[4,144,128]{2,1,0:T(8,128)(2,1)S(1)}, bf16[4,144,128]{2,1,0:T(8,128)(2,1)S(1)}, u32[]{:S(2)}, u32[]{:S(2)}) collective-permute-start(bf16[4,144,128]{2,1,0:T(8,128)(2,1)S(1)} %pad_maximum_fusion.1.source), channel_id=1, source_target_pairs={{0,2},{2,0},{1,3},{3,1},{4,6},{6,4},{5,7},{7,5},{8,10},{10,8},{9,1... | collective-permute-start | bytes 442376 | tf_op jit(solution)/shard_map/ppermute | solution.py:260
  13.4 3.6 %copy-start.5 = (f32[2,64]{1,0:T(2,128)S(1)}, f32[2,64]{1,0:T(2,128)}, u32[]{:S(2)}) copy-start(f32[2,64]{1,0:T(2,128)} %param.12) | copy-start | bytes 1540
  13.4 3.6 %copy-start.6 = (f32[2,64]{1,0:T(2,128)S(1)}, f32[2,64]{1,0:T(2,128)}, u32[]{:S(2)}) copy-start(f32[2,64]{1,0:T(2,128)} %param.9) | copy-start | bytes 1540
  13.5 5.0 %collective-permute-start.6 = (bf16[2,6,64,128]{3,2,1,0:T(8,128)(2,1)S(1)}, bf16[2,6,64,128]{3,2,1,0:T(8,128)(2,1)S(1)}, u32[]{:S(2)}, u32[]{:S(2)}) collective-permute-start(bf16[2,6,64,128]{3,2,1,0:T(8,128)(2,1)S(1)} %pad_maximum_fusion.own), channel_id=1, source_target_pairs={{0,1},{1,0},{2,3},{3,2},{4,5},{5,4},{6,7},{7,6},{8,9},{9,8},{10,11... | collective-permute-start | bytes 589832 | tf_op jit(solution)/shard_map/ppermute | solution.py:260
  13.6 5.7 %collective-permute-start.8 = (bf16[4,144,128]{2,1,0:T(8,128)(2,1)S(1)}, bf16[4,144,128]{2,1,0:T(8,128)(2,1)S(1)}, u32[]{:S(2)}, u32[]{:S(2)}) collective-permute-start(bf16[4,144,128]{2,1,0:T(8,128)(2,1)S(1)} %pad_maximum_fusion.1.source), channel_id=1, source_target_pairs={{0,1},{1,0},{2,3},{3,2},{4,5},{5,4},{6,7},{7,6},{8,9},{9,8},{10,11... | collective-permute-start | bytes 442376 | tf_op jit(solution)/shard_map/ppermute | solution.py:260
  17.1 5.2 %collective-permute-start.5 = (bf16[4,144,128]{2,1,0:T(8,128)(2,1)S(1)}, bf16[4,144,128]{2,1,0:T(8,128)(2,1)S(1)}, u32[]{:S(2)}, u32[]{:S(2)}) collective-permute-start(bf16[4,144,128]{2,1,0:T(8,128)(2,1)S(1)} %collective-permute-done.4.source), channel_id=1, source_target_pairs={{0,1},{1,0},{2,3},{3,2},{4,5},{5,4},{6,7},{7,6},{8,9},{9,8},{10,11... | collective-permute-start | bytes 442376 | tf_op jit(solution)/shard_map/ppermute | solution.py:260
  17.1 1.4 %copy-start.1 = (s32[48]{0:T(128)S(1)}, s32[48]{0:T(128)}, u32[]{:S(2)}) copy-start(s32[48]{0:T(128)} %param.8) | copy-start | bytes 580
  17.1 1.4 %collective-permute-start.7 = (f32[4,64]{1,0:T(4,128)S(1)}, f32[4,64]{1,0:T(4,128)S(1)}, u32[]{:S(2)}, u32[]{:S(2)}) collective-permute-start(f32[4,64]{1,0:T(4,128)S(1)} %pad_maximum_fusion.2.own_gains), channel_id=1, source_target_pairs={{0,1},{1,0},{2,3},{3,2},{4,5},{5,4},{6,7},{7,6},{8,9},{9,8},{10,11... | collective-permute-start | bytes 3080 | tf_op jit(solution)/shard_map/ppermute | solution.py:260

commit v3 on v2

--- a/solution.py
+++ b/solution.py
@@ -18,9 +18,10 @@
     return jnp.dot(x.astype(BF16), w, preferred_element_type=F32)
 
 
-def lane_norm(x, gain, ones):
+def lane_norm(x, gain, ones=None):
     d = x - jnp.mean(x, axis=-1, keepdims=True)
-    return d * lax.rsqrt(dot(d * d, ones) + EPSILON) * gain
+    var = jnp.mean(d * d, axis=-1, keepdims=True) if ones is None else dot(d * d, ones)
+    return d * lax.rsqrt(var + EPSILON) * gain
 
 
 def gated(x, w):
@@ -55,8 +56,9 @@
     for u in range(2):
         for p in range(6):
             mine, theirs = own[u, p].astype(F32) * 0.5, other[u, p].astype(F32) * 0.5
-            first = jnp.where(core == 0, mine, theirs)
-            second = jnp.where(core == 0, theirs, mine)
+            natural = (core == 0) | (u == 1 and p >= 4)
+            first = jnp.where(natural, mine, theirs)
+            second = jnp.where(natural, theirs, mine)
             full = jnp.transpose(jnp.concatenate([first, second], axis=0)).astype(BF16)
             if p < 2:
                 wleft[u, :, p * 2 * half : (p + 1) * 2 * half] = full
@@ -239,8 +241,8 @@
         r = right1[pl.ds(pl.multiple_of(k * cols, 8), cols), :]
         return tuple(acc + left1[pl.ds(k * ipad + i, 1), :] * r for i, acc in enumerate(accs))
 
-    accs = lax.fori_loop(0, res, tri1_block, tuple(jnp.zeros((cols, ch), F32) for _ in range(rows)), unroll=4)
-    tn = lane_norm(jnp.concatenate(accs, axis=0), gain_out[1:2], ones)
+    accs = lax.fori_loop(0, res, tri1_block, tuple(jnp.zeros((cols, ch), F32) for _ in range(rows)), unroll=12 if res % 12 == 0 else 4)
+    tn = lane_norm(jnp.concatenate(accs, axis=0), gain_out[1:2])
     ns, us, ms = [], [], []
     for i in range(rows):
         local = (at.core ^ (i // half)) * at.part + i % half
@@ -251,7 +253,7 @@
     gate = (jnp.tanh(dot(jnp.concatenate(ns, axis=0), wgate[1])) + 1.0) * jnp.concatenate(ms, axis=0)
     part = ch // 2
     before = pltpu.roll(jnp.concatenate(us, axis=0), at.core * part, 1)
-    moved = before + pltpu.roll(gate * dot(tn, wout[1]), at.core * part, 1)
+    moved = before + gate * dot(tn, wout[1])
     out[...] = pair[...] + moved[:, :part].reshape(rows, cols, part)
 
 

time: 27.7 us -> 27.5 us (level)
  no operation moved by 1% of the time
where the time goes in v3:
time: 27.5 us; the launch traced here: 27.4 us
  Pallas kernels  9.05 us (33%)
  starting transfers between devices  8.84 us (32%)
  waiting for transfers between devices  8.35 us (30%)
  local copies, waits for them, and re-layouts  0.94 us (3%)
    pallas_call x8, Pallas kernels, call(): pl.pallas_call(kernel, out_shape=out_shape, scratch_shapes=list(scratch),...  9.05 us
    ppermute x9, starting transfers between devices, swap(): return lax.ppermute(x, axis, [(i, i ^ mask) for i in range(size)])  8.84 us
    ppermute x9, waiting for transfers between devices, swap(): return lax.ppermute(x, axis, [(i, i ^ mask) for i in range(size)])  8.35 us
    unnamed x14, local copies, waits for them, and re-layouts  0.94 us
  transfers between devices with their start and end apart: 9, of which 5 were waited for; matrix products, arithmetic and copies ran while one was open for 0% of the time, Pallas kernels for 14%

profile of v3, /device:TPU:0, one launch (start us, length us, event | category | flops | bytes accessed | tf_op | source)
XLA Modules:
  0.0 27.4 jit_solution(17610318333595901889)
XLA Ops:
  0.0 0.5 %collective-permute-start = (f32[12,24,64]{2,1,0:T(8,128)}, f32[12,24,64]{2,1,0:T(8,128)S(1)}, u32[]{:S(2)}, u32[]{:S(2)}) collective-permute-start(f32[12,24,64]{2,1,0:T(8,128)} %bitcast.15), channel_id=1, source_target_pairs={{0,1},{1,0},{2,3},{3,2},{4,5},{5,4},{6,7},{7,6},{8,9},{9,8},{10,11... | collective-permute-start | bytes 221192 | tf_op jit(solution)/shard_map/ppermute | solution.py:262
  0.5 0.0 copy-start
  0.5 0.9 %copy-done = f32[64,12,24]{0,2,1:T(8,128)S(1)} copy-done((f32[64,12,24]{0,2,1:T(8,128)S(1)}, f32[64,12,24]{0,2,1:T(8,128)}, u32[]{:S(2)}) %copy-start) | copy-done | bytes 73752
  1.4 0.3 %collective-permute-done.other = f32[12,24,64]{2,1,0:T(8,128)S(1)} collective-permute-done((f32[12,24,64]{2,1,0:T(8,128)}, f32[12,24,64]{2,1,0:T(8,128)S(1)}, u32[]{:S(2)}, u32[]{:S(2)}) %collective-permute-start) | collective-permute-done | bytes 73760 | tf_op jit(solution)/shard_map/ppermute | solution.py:262
  1.7 0.2 shard_map.74
  1.9 5.0 %collective-permute-start.3 = (bf16[144,128]{1,0:T(8,128)(2,1)S(1)}, bf16[144,128]{1,0:T(8,128)(2,1)S(1)}, u32[]{:S(2)}, u32[]{:S(2)}) collective-permute-start(bf16[144,128]{1,0:T(8,128)(2,1)S(1)} %shard_map.74), channel_id=1, source_target_pairs={{0,12},{4,8},{8,4},{12,0},{1,13},{5,9},{9,5},{13,1},{2,14},{6,10},... | collective-permute-start | bytes 110600 | tf_op jit(solution)/shard_map/ppermute | solution.py:262
  7.0 0.0 collective-permute-start.2
  7.0 0.6 %collective-permute-start.1 = (bf16[144,128]{1,0:T(8,128)(2,1)S(1)}, bf16[144,128]{1,0:T(8,128)(2,1)S(1)}, u32[]{:S(2)}, u32[]{:S(2)}) collective-permute-start(bf16[144,128]{1,0:T(8,128)(2,1)S(1)} %shard_map.74), channel_id=1, source_target_pairs={{0,4},{4,0},{8,12},{12,8},{1,5},{5,1},{9,13},{13,9},{2,6},{6,2},{1... | collective-permute-start | bytes 110600 | tf_op jit(solution)/shard_map/ppermute | solution.py:262
  7.6 1.3 %collective-permute-done.3 = bf16[144,128]{1,0:T(8,128)(2,1)S(1)} collective-permute-done((bf16[144,128]{1,0:T(8,128)(2,1)S(1)}, bf16[144,128]{1,0:T(8,128)(2,1)S(1)}, u32[]{:S(2)}, u32[]{:S(2)}) %collective-permute-start.3) | collective-permute-done | bytes 36896 | tf_op jit(solution)/shard_map/ppermute | solution.py:262
  8.9 2.9 %collective-permute-done.2 = bf16[144,128]{1,0:T(8,128)(2,1)S(1)} collective-permute-done((bf16[144,128]{1,0:T(8,128)(2,1)S(1)}, bf16[144,128]{1,0:T(8,128)(2,1)S(1)}, u32[]{:S(2)}, u32[]{:S(2)}) %collective-permute-start.2) | collective-permute-done | bytes 36896 | tf_op jit(solution)/shard_map/ppermute | solution.py:262
  11.8 0.0 collective-permute-done.1
  11.8 0.0 copy-start.2
  11.8 0.0 copy-start.3
  11.8 0.0 copy-start.4
  11.9 1.6 %collective-permute-start.4 = (bf16[4,144,128]{2,1,0:T(8,128)(2,1)S(1)}, bf16[4,144,128]{2,1,0:T(8,128)(2,1)S(1)}, u32[]{:S(2)}, u32[]{:S(2)}) collective-permute-start(bf16[4,144,128]{2,1,0:T(8,128)(2,1)S(1)} %pad_maximum_fusion.1.source), channel_id=1, source_target_pairs={{0,2},{2,0},{1,3},{3,1},{4,6},{6,4},{5,7},{7,5},{8,10},{10,8},{9,1... | collective-permute-start | bytes 442376 | tf_op jit(solution)/shard_map/ppermute | solution.py:262
  13.4 0.0 copy-done.2
  13.4 0.0 copy-done.3
  13.4 0.0 copy-done.4
  13.4 0.0 copy-start.5
  13.4 0.0 copy-start.6
  13.5 0.1 collective-permute-start.6
  13.6 0.5 %collective-permute-start.8 = (bf16[4,144,128]{2,1,0:T(8,128)(2,1)S(1)}, bf16[4,144,128]{2,1,0:T(8,128)(2,1)S(1)}, u32[]{:S(2)}, u32[]{:S(2)}) collective-permute-start(bf16[4,144,128]{2,1,0:T(8,128)(2,1)S(1)} %pad_maximum_fusion.1.source), channel_id=1, source_target_pairs={{0,1},{1,0},{2,3},{3,2},{4,5},{5,4},{6,7},{7,6},{8,9},{9,8},{10,11... | collective-permute-start | bytes 442376 | tf_op jit(solution)/shard_map/ppermute | solution.py:262
  14.1 3.0 %collective-permute-done.4.source = bf16[4,144,128]{2,1,0:T(8,128)(2,1)S(1)} collective-permute-done((bf16[4,144,128]{2,1,0:T(8,128)(2,1)S(1)}, bf16[4,144,128]{2,1,0:T(8,128)(2,1)S(1)}, u32[]{:S(2)}, u32[]{:S(2)}) %collective-permute-start.4) | collective-permute-done | bytes 147488 | tf_op jit(solution)/shard_map/ppermute | solution.py:262
  17.1 0.0 collective-permute-start.5
  17.1 0.0 copy-done.5
  17.1 0.0 copy-done.6
  17.1 0.0 copy-start.1
  17.1 0.6 %collective-permute-start.7 = (f32[4,64]{1,0:T(4,128)S(1)}, f32[4,64]{1,0:T(4,128)S(1)}, u32[]{:S(2)}, u32[]{:S(2)}) collective-permute-start(f32[4,64]{1,0:T(4,128)S(1)} %pad_maximum_fusion.2.own_gains), channel_id=1, source_target_pairs={{0,1},{1,0},{2,3},{3,2},{4,5},{5,4},{6,7},{7,6},{8,9},{9,8},{10,11... | collective-permute-start | bytes 3080 | tf_op jit(solution)/shard_map/ppermute | solution.py:262
  17.7 0.8 %collective-permute-done.7.other_gains = f32[4,64]{1,0:T(4,128)S(1)} collective-permute-done((f32[4,64]{1,0:T(4,128)S(1)}, f32[4,64]{1,0:T(4,128)S(1)}, u32[]{:S(2)}, u32[]{:S(2)}) %collective-permute-start.7) | collective-permute-done | bytes 1056 | tf_op jit(solution)/shard_map/ppermute | solution.py:262
  18.5 0.0 collective-permute-done.6.other
  18.5 0.0 copy-done.1
  18.5 0.4 %shard_map.75 = (bf16[2,128,256]{2,1,0:T(8,128)(2,1)S(1)}, bf16[2,128,256]{2,1,0:T(8,128)(2,1)S(1)}, bf16[2,128,128]{2,1,0:T(8,128)(2,1)S(1)}, bf16[2,128,128]{2...) custom-call(bf16[2,6,64,128]{3,2,1,0:T(8,128)(2,1)S(1)} %pad_maximum_fusion.own, ...), custom_call_target="tpu_custom_call" | custom-call | flops 1048576 | bytes 65536 | tf_op jit(solution)/shard_map/pallas_call | solution.py:266
  18.9 0.4 %shard_map.76 = (f32[584,128]{1,0:T(8,128)S(1)}, f32[584,128]{1,0:T(8,128)S(1)}, f32[576,128]{1,0:T(8,128)S(1)}, f32[432,128]{1,0:T(8,128)S(1)}) custom-call(bf16[4,144,128]{2,1,0:T(8,128)(2,1)S(1)} %pad_maximum_fusion.1.source, f32[56,128]{1,0:T(8,128)S(1)} %get-tuple-element.27.mask, f32[4,128]{1,0:T(4,128)S(1)} %get-tuple-element.28.gains, ...), custom_call_target="tpu_custom_call" | custom-call | flops 16777216 | bytes 65536 | tf_op jit(solution)/shard_map/pallas_call | solution.py:266
  19.3 0.0 collective-permute-done.8.source
  19.3 0.4 %shard_map.77 = (f32[584,128]{1,0:T(8,128)S(1)}, f32[584,128]{1,0:T(8,128)S(1)}, f32[576,128]{1,0:T(8,128)S(1)}, f32[960,128]{1,0:T(8,128)S(1)}) custom-call(bf16[4,144,128]{2,1,0:T(8,128)(2,1)S(1)} %collective-permute-done.8.source, f32[432,128]{1,0:T(8,128)S(1)} %get-tuple-element.32.right_own, f32[56,128]{1,0:T(8,128)S(1)} %get-tuple-element.27.mask, ...), custom_call_target="tpu_custom_call" | custom-call | flops 16777216 | bytes 65536 | tf_op jit(solution)/shard_map/pallas_call | solution.py:266
  19.7 0.5 %shard_map.79 = (f32[584,128]{1,0:T(8,128)S(1)}, f32[584,128]{1,0:T(8,128)S(1)}, f32[576,128]{1,0:T(8,128)S(1)}, f32[432,128]{1,0:T(8,128)S(1)}, f32[1152,128]{1,0:T(8,128)S(1)}) custom-call(bf16[4,144,128]{2,1,0:T(8,128)(2,1)S(1)} %collective-permute-done.4.source, f32[584,128]{1,0:T(8,128)S(1)} %get-tuple-element.34.near_own.near_normed_own, ...), custom_call_target="tpu_custom_call" | custom-call | flops 16777216 | bytes 65536 | tf_op jit(solution)/shard_map/pallas_call | solution.py:266
  20.2 2.0 %shard_map.78.near_tri = f32[1920,128]{1,0:T(8,128)S(1)} custom-call(f32[576,128]{1,0:T(8,128)S(1)} %get-tuple-element.36.left_own, f32[576,128]{1,0:T(8,128)S(1)} %get-tuple-element.37.left_other, f32[960,128]{1,0:T(8,128)S(1)} %get-tuple-element.38.rightt), custom_call_target="tpu_custom_call" | custom-call | flops 67108864 | bytes 65536 | tf_op jit(solution)/shard_map/pallas_call | solution.py:266
  22.3 0.0 collective-permute-done.5.source
  22.3 5.1 %shard_map.80 = f32[12,24,64]{2,1,0:T(8,128)} custom-call(bf16[4,144,128]{2,1,0:T(8,128)(2,1)S(1)} %collective-permute-done.5.source, f32[584,128]{1,0:T(8,128)S(1)} %get-tuple-element.31.near_raws_own, f32[584,128]{1,0:T(8,128)S(1)} %get-tuple-element.33.near_raws_other, f32[584,128]{1,0:T(8,128)S(1)} %get-tuple-element.34.near_own.near_normed_own, ...), custom_call_target="tpu_custom_call" | custom-call | flops 1048576 | bytes 65536 | tf_op jit(solution)/shard_map/pallas_call | solution.py:266
  (4 shorter events, 0.1 us)
Async XLA Ops:
  0.0 1.7 %collective-permute-start = (f32[12,24,64]{2,1,0:T(8,128)}, f32[12,24,64]{2,1,0:T(8,128)S(1)}, u32[]{:S(2)}, u32[]{:S(2)}) collective-permute-start(f32[12,24,64]{2,1,0:T(8,128)} %bitcast.15), channel_id=1, source_target_pairs={{0,1},{1,0},{2,3},{3,2},{4,5},{5,4},{6,7},{7,6},{8,9},{9,8},{10,11... | collective-permute-start | bytes 221192 | tf_op jit(solution)/shard_map/ppermute | solution.py:262
  0.5 0.9 %copy-start = (f32[64,12,24]{0,2,1:T(8,128)S(1)}, f32[64,12,24]{0,2,1:T(8,128)}, u32[]{:S(2)}) copy-start(f32[64,12,24]{0,2,1:T(8,128)} %param.7) | copy-start | bytes 221188
  1.9 7.0 %collective-permute-start.3 = (bf16[144,128]{1,0:T(8,128)(2,1)S(1)}, bf16[144,128]{1,0:T(8,128)(2,1)S(1)}, u32[]{:S(2)}, u32[]{:S(2)}) collective-permute-start(bf16[144,128]{1,0:T(8,128)(2,1)S(1)} %shard_map.74), channel_id=1, source_target_pairs={{0,12},{4,8},{8,4},{12,0},{1,13},{5,9},{9,5},{13,1},{2,14},{6,10},... | collective-permute-start | bytes 110600 | tf_op jit(solution)/shard_map/ppermute | solution.py:262
  7.0 4.9 %collective-permute-start.2 = (bf16[144,128]{1,0:T(8,128)(2,1)S(1)}, bf16[144,128]{1,0:T(8,128)(2,1)S(1)}, u32[]{:S(2)}, u32[]{:S(2)}) collective-permute-start(bf16[144,128]{1,0:T(8,128)(2,1)S(1)} %shard_map.74), channel_id=1, source_target_pairs={{0,8},{4,12},{8,0},{12,4},{1,9},{5,13},{9,1},{13,5},{2,10},{6,14},... | collective-permute-start | bytes 110600 | tf_op jit(solution)/shard_map/ppermute | solution.py:262
  7.0 4.9 %collective-permute-start.1 = (bf16[144,128]{1,0:T(8,128)(2,1)S(1)}, bf16[144,128]{1,0:T(8,128)(2,1)S(1)}, u32[]{:S(2)}, u32[]{:S(2)}) collective-permute-start(bf16[144,128]{1,0:T(8,128)(2,1)S(1)} %shard_map.74), channel_id=1, source_target_pairs={{0,4},{4,0},{8,12},{12,8},{1,5},{5,1},{9,13},{13,9},{2,6},{6,2},{1... | collective-permute-start | bytes 110600 | tf_op jit(solution)/shard_map/ppermute | solution.py:262
  11.8 1.6 %copy-start.2 = (bf16[2,4,128,64]{2,3,1,0:T(8,128)(2,1)S(1)}, bf16[2,4,128,64]{2,3,1,0:T(8,128)(2,1)}, u32[]{:S(2)}) copy-start(bf16[2,4,128,64]{2,3,1,0:T(8,128)(2,1)} %param.10) | copy-start | bytes 393220
  11.8 1.6 %copy-start.3 = (bf16[2,128,64]{1,2,0:T(8,128)(2,1)S(1)}, bf16[2,128,64]{1,2,0:T(8,128)(2,1)}, u32[]{:S(2)}) copy-start(bf16[2,128,64]{1,2,0:T(8,128)(2,1)} %param.13) | copy-start | bytes 98308
  11.8 1.6 %copy-start.4 = (bf16[2,128,64]{1,2,0:T(8,128)(2,1)S(1)}, bf16[2,128,64]{1,2,0:T(8,128)(2,1)}, u32[]{:S(2)}) copy-start(bf16[2,128,64]{1,2,0:T(8,128)(2,1)} %param.11) | copy-start | bytes 98308
  11.9 5.2 %collective-permute-start.4 = (bf16[4,144,128]{2,1,0:T(8,128)(2,1)S(1)}, bf16[4,144,128]{2,1,0:T(8,128)(2,1)S(1)}, u32[]{:S(2)}, u32[]{:S(2)}) collective-permute-start(bf16[4,144,128]{2,1,0:T(8,128)(2,1)S(1)} %pad_maximum_fusion.1.source), channel_id=1, source_target_pairs={{0,2},{2,0},{1,3},{3,1},{4,6},{6,4},{5,7},{7,5},{8,10},{10,8},{9,1... | collective-permute-start | bytes 442376 | tf_op jit(solution)/shard_map/ppermute | solution.py:262
  13.4 3.6 %copy-start.5 = (f32[2,64]{1,0:T(2,128)S(1)}, f32[2,64]{1,0:T(2,128)}, u32[]{:S(2)}) copy-start(f32[2,64]{1,0:T(2,128)} %param.12) | copy-start | bytes 1540
  13.4 3.6 %copy-start.6 = (f32[2,64]{1,0:T(2,128)S(1)}, f32[2,64]{1,0:T(2,128)}, u32[]{:S(2)}) copy-start(f32[2,64]{1,0:T(2,128)} %param.9) | copy-start | bytes 1540
  13.5 5.0 %collective-permute-start.6 = (bf16[2,6,64,128]{3,2,1,0:T(8,128)(2,1)S(1)}, bf16[2,6,64,128]{3,2,1,0:T(8,128)(2,1)S(1)}, u32[]{:S(2)}, u32[]{:S(2)}) collective-permute-start(bf16[2,6,64,128]{3,2,1,0:T(8,128)(2,1)S(1)} %pad_maximum_fusion.own), channel_id=1, source_target_pairs={{0,1},{1,0},{2,3},{3,2},{4,5},{5,4},{6,7},{7,6},{8,9},{9,8},{10,11... | collective-permute-start | bytes 589832 | tf_op jit(solution)/shard_map/ppermute | solution.py:262
  13.6 5.7 %collective-permute-start.8 = (bf16[4,144,128]{2,1,0:T(8,128)(2,1)S(1)}, bf16[4,144,128]{2,1,0:T(8,128)(2,1)S(1)}, u32[]{:S(2)}, u32[]{:S(2)}) collective-permute-start(bf16[4,144,128]{2,1,0:T(8,128)(2,1)S(1)} %pad_maximum_fusion.1.source), channel_id=1, source_target_pairs={{0,1},{1,0},{2,3},{3,2},{4,5},{5,4},{6,7},{7,6},{8,9},{9,8},{10,11... | collective-permute-start | bytes 442376 | tf_op jit(solution)/shard_map/ppermute | solution.py:262
  17.1 5.2 %collective-permute-start.5 = (bf16[4,144,128]{2,1,0:T(8,128)(2,1)S(1)}, bf16[4,144,128]{2,1,0:T(8,128)(2,1)S(1)}, u32[]{:S(2)}, u32[]{:S(2)}) collective-permute-start(bf16[4,144,128]{2,1,0:T(8,128)(2,1)S(1)} %collective-permute-done.4.source), channel_id=1, source_target_pairs={{0,1},{1,0},{2,3},{3,2},{4,5},{5,4},{6,7},{7,6},{8,9},{9,8},{10,11... | collective-permute-start | bytes 442376 | tf_op jit(solution)/shard_map/ppermute | solution.py:262
  17.1 1.4 %copy-start.1 = (s32[48]{0:T(128)S(1)}, s32[48]{0:T(128)}, u32[]{:S(2)}) copy-start(s32[48]{0:T(128)} %param.8) | copy-start | bytes 580
  17.1 1.4 %collective-permute-start.7 = (f32[4,64]{1,0:T(4,128)S(1)}, f32[4,64]{1,0:T(4,128)S(1)}, u32[]{:S(2)}, u32[]{:S(2)}) collective-permute-start(f32[4,64]{1,0:T(4,128)S(1)} %pad_maximum_fusion.2.own_gains), channel_id=1, source_target_pairs={{0,1},{1,0},{2,3},{3,2},{4,5},{5,4},{6,7},{7,6},{8,9},{9,8},{10,11... | collective-permute-start | bytes 3080 | tf_op jit(solution)/shard_map/ppermute | solution.py:262

commit v4 on v3

--- a/solution.py
+++ b/solution.py
@@ -138,27 +138,24 @@
                 rightt[pl.ds(slot, cols, stride=span), :] = right[first : first + cols, :]
 
 
-def triangle_phase(at, left_own, left_other, rightt, tri, start):
+def triangle_phase(at, left, rightt, tri, base, start):
     cols, span = at.cols, at.span
     ch = rightt.shape[1]
     count = 4
-    for left, base in ((left_own, 0), (left_other, at.part)):
-
-        def tri_block(n, carry, left=left, base=base):
-            def add(k, accs):
-                r = rightt[pl.ds(pl.multiple_of(k * span, 8), span), :]
-                return tuple(
-                    acc + left[pl.ds((n * count + q) * cols + k, 1), :] * r for q, acc in enumerate(accs)
-                )
-
-            where = [pl.ds(pl.multiple_of((base + n * count + q) * span, 8), span) for q in range(count)]
-            accs = tuple(jnp.zeros((span, ch), F32) if start is None else start[w, :] for w in where)
-            accs = lax.fori_loop(0, cols, add, accs, unroll=min(cols, 24))
-            for w, acc in zip(where, accs):
-                tri[w, :] = acc
-            return carry
-
-        lax.fori_loop(0, at.part // count, tri_block, 0)
+
+    def tri_block(n, carry):
+        def add(k, accs):
+            r = rightt[pl.ds(pl.multiple_of(k * span, 8), span), :]
+            return tuple(acc + left[pl.ds((n * count + q) * cols + k, 1), :] * r for q, acc in enumerate(accs))
+
+        where = [pl.multiple_of((n * count + q) * span, 8) for q in range(count)]
+        accs = tuple(jnp.zeros((span, ch), F32) if start is None else start[pl.ds(w, span), :] for w in where)
+        accs = lax.fori_loop(0, cols, add, accs, unroll=min(cols, 24))
+        for w, acc in zip(where, accs):
+            tri[pl.ds(base * span + w, span), :] = acc
+        return carry
+
+    lax.fori_loop(0, at.part // count, tri_block, 0, unroll=3 if at.part // count % 3 == 0 else 1)
 
 
 def near_own_kernel(source, mask, gains, wleft, wright, raw, normed, left, right, *, place):
@@ -174,8 +171,8 @@
     place_right(at, right_own, right, rightt)
 
 
-def near_triangle_kernel(left_own, left_other, rightt, tri, *, place):
-    triangle_phase(Place(*place), left_own, left_other, rightt, tri, None)
+def near_triangle_kernel(left, rightt, tri, *, place):
+    triangle_phase(Place(*place), left, rightt, tri, 0, None)
 
 
 def far_own_kernel(
@@ -189,7 +186,7 @@
 
 
 def far_kernel(
-    source, near_raws_own, near_raws_other, near_normed_own, near_normed_other, near_tri,
+    source, near_raws_own, near_raws_other, near_normed_own, near_normed_other, near_tri_own, near_tri_other,
     raw_own, normed_own, left_own, right_own, near_gate,
     mask, gains, wleft, wright, wgate, wout, pair, out,
     raw_other, normed_other, left_other, right_other, rightt, tri, first_update, znext, right1, left1, *, place,
@@ -201,7 +198,8 @@
         at, source, mask, gains, wleft, wright, raw_other, normed_other, left_other, right_other, 1 - at.col_block
     )
     place_right(at, right_own, right_other, rightt)
-    triangle_phase(at, left_own, left_other, rightt, tri, near_tri)
+    triangle_phase(at, left_own, rightt, tri, 0, near_tri_own)
+    triangle_phase(at, left_other, rightt, tri, at.part, near_tri_other)
     ones = jnp.full((ch, ch), 1.0 / ch, BF16)
     gain_in, gain_out = gains[0:2, :], gains[2:4, :]
 
@@ -316,7 +314,9 @@
         vmem_mib=8,
     )
     near = jnp.stack(column)
-    far = swap(near, "gy")
+    far_first = swap(message, "gy")
+    far_rest = swap(jnp.stack(column[1:]), "gy")
+    far = jnp.concatenate([far_first[None], far_rest], axis=0)
     near_other = swap(near, "gz")
     far_other = swap(far, "gz")
     part_pairs = pairs // 2
@@ -336,12 +336,16 @@
         scratch=[vmem(right_rows)],
         flops=2**24,
     )
-    near_tri = call(
-        functools.partial(near_triangle_kernel, place=place),
-        wide(res * span),
-        left_own, left_other, near_right,
-        flops=2**26,
-    )
+    near_tris = []
+    for left in (left_own, left_other):
+        near_tris.append(
+            call(
+                functools.partial(near_triangle_kernel, place=place),
+                wide(res // 2 * span),
+                left, near_right,
+                flops=2**25,
+            )
+        )
     *far_parts, near_gate = call(
         functools.partial(far_own_kernel, place=place),
         part_shapes + [wide(pairs)],
@@ -351,7 +355,7 @@
     result = call(
         functools.partial(far_kernel, place=place),
         jax.ShapeDtypeStruct(tile.shape, F32),
-        far_other, raw_own, raw_other, normed_own, normed_other, near_tri, *far_parts, near_gate,
+        far_other, raw_own, raw_other, normed_own, normed_other, *near_tris, *far_parts, near_gate,
         *parameters, wgate, wout, kept_tile,
         scratch=[
             vmem(part_pairs + 8),

time: 27.5 us -> 27.2 us (0.989)
  waiting for transfers between devices: 8.35 us -> 6.99 us
  starting transfers between devices: 8.84 us -> 9.69 us
  local copies, waits for them, and re-layouts: 0.94 us -> 1.52 us
  Pallas kernels: 9.05 us -> 8.62 us
    ppermute x9 -> x10, waiting for transfers between devices: 8.35 us -> 6.99 us  [swap(): return lax.ppermute(x, axis, [(i, i ^ mask) for i in range(size)])]
    ppermute x9 -> x10, starting transfers between devices: 8.84 us -> 9.69 us  [swap(): return lax.ppermute(x, axis, [(i, i ^ mask) for i in range(size)])]
    unnamed x14, local copies, waits for them, and re-layouts: 0.94 us -> 1.52 us
    pallas_call x8 -> x9, Pallas kernels: 9.05 us -> 8.62 us  [call(): pl.pallas_call(kernel, out_shape=out_shape, scratch_shapes=list(scratch),...]
  transfers between devices with their start and end apart: 9 -> 10, of which waited for: 5 -> 4; matrix products, arithmetic and copies ran while one was open for 0% -> 0% of each run, Pallas kernels for 14% -> 13%
where the time goes in v4:
time: 27.2 us; the launch traced here: 27 us
  starting transfers between devices  9.69 us (36%)
  Pallas kernels  8.62 us (32%)
  waiting for transfers between devices  6.99 us (26%)
  local copies, waits for them, and re-layouts  1.52 us (6%)
    ppermute x10, starting transfers between devices, swap(): return lax.ppermute(x, axis, [(i, i ^ mask) for i in range(size)])  9.69 us
    pallas_call x9, Pallas kernels, call(): pl.pallas_call(kernel, out_shape=out_shape, scratch_shapes=list(scratch),...  8.62 us
    ppermute x10, waiting for transfers between devices, swap(): return lax.ppermute(x, axis, [(i, i ^ mask) for i in range(size)])  6.99 us
    unnamed x14, local copies, waits for them, and re-layouts  1.52 us
  transfers between devices with their start and end apart: 10, of which 4 were waited for; matrix products, arithmetic and copies ran while one was open for 0% of the time, Pallas kernels for 13%

profile of v4, /device:TPU:0, one launch (start us, length us, event | category | flops | bytes accessed | tf_op | source)
XLA Modules:
  0.0 27.0 jit_solution(8800926661498769096)
XLA Ops:
  0.0 0.5 %collective-permute-start = (f32[12,24,64]{2,1,0:T(8,128)}, f32[12,24,64]{2,1,0:T(8,128)S(1)}, u32[]{:S(2)}, u32[]{:S(2)}) collective-permute-start(f32[12,24,64]{2,1,0:T(8,128)} %bitcast.16), channel_id=1, source_target_pairs={{0,1},{1,0},{2,3},{3,2},{4,5},{5,4},{6,7},{7,6},{8,9},{9,8},{10,11... | collective-permute-start | bytes 221192 | tf_op jit(solution)/shard_map/ppermute | solution.py:260
  0.5 0.0 copy-start
  0.5 0.9 %copy-done = f32[64,12,24]{0,2,1:T(8,128)S(1)} copy-done((f32[64,12,24]{0,2,1:T(8,128)S(1)}, f32[64,12,24]{0,2,1:T(8,128)}, u32[]{:S(2)}) %copy-start) | copy-done | bytes 73752
  1.4 0.3 %collective-permute-done.other = f32[12,24,64]{2,1,0:T(8,128)S(1)} collective-permute-done((f32[12,24,64]{2,1,0:T(8,128)}, f32[12,24,64]{2,1,0:T(8,128)S(1)}, u32[]{:S(2)}, u32[]{:S(2)}) %collective-permute-start) | collective-permute-done | bytes 73760 | tf_op jit(solution)/shard_map/ppermute | solution.py:260
  1.7 0.0 copy-start.2
  1.7 0.0 copy-start.3
  1.7 0.0 copy-start.4
  1.7 0.2 shard_map.74
  2.0 5.0 %collective-permute-start.4 = (bf16[144,128]{1,0:T(8,128)(2,1)S(1)}, bf16[144,128]{1,0:T(8,128)(2,1)S(1)}, u32[]{:S(2)}, u32[]{:S(2)}) collective-permute-start(bf16[144,128]{1,0:T(8,128)(2,1)S(1)} %shard_map.74), channel_id=1, source_target_pairs={{0,12},{4,8},{8,4},{12,0},{1,13},{5,9},{9,5},{13,1},{2,14},{6,10},... | collective-permute-start | bytes 110600 | tf_op jit(solution)/shard_map/ppermute | solution.py:260
  7.0 0.0 collective-permute-start.3
  7.0 0.6 %collective-permute-start.2 = (bf16[144,128]{1,0:T(8,128)(2,1)S(1)}, bf16[144,128]{1,0:T(8,128)(2,1)S(1)}, u32[]{:S(2)}, u32[]{:S(2)}) collective-permute-start(bf16[144,128]{1,0:T(8,128)(2,1)S(1)} %shard_map.74), channel_id=1, source_target_pairs={{0,4},{4,0},{8,12},{12,8},{1,5},{5,1},{9,13},{13,9},{2,6},{6,2},{1... | collective-permute-start | bytes 110600 | tf_op jit(solution)/shard_map/ppermute | solution.py:260
  7.6 0.0 copy-done.2
  7.6 0.0 copy-done.3
  7.6 0.0 copy-done.4
  7.7 0.1 collective-permute-start.7
  7.7 1.7 %collective-permute-start.1 = (bf16[144,128]{1,0:T(8,128)(2,1)S(1)}, bf16[144,128]{1,0:T(8,128)(2,1)S(1)}, u32[]{:S(2)}, u32[]{:S(2)}) collective-permute-start(bf16[144,128]{1,0:T(8,128)(2,1)S(1)} %shard_map.74), channel_id=1, source_target_pairs={{0,2},{2,0},{1,3},{3,1},{4,6},{6,4},{5,7},{7,5},{8,10},{10,8},{9,1... | collective-permute-start | bytes 110600 | tf_op jit(solution)/shard_map/ppermute | solution.py:260
  9.4 0.0 collective-permute-done.4
  9.4 2.4 %collective-permute-done.3 = bf16[144,128]{1,0:T(8,128)(2,1)S(1)} collective-permute-done((bf16[144,128]{1,0:T(8,128)(2,1)S(1)}, bf16[144,128]{1,0:T(8,128)(2,1)S(1)}, u32[]{:S(2)}, u32[]{:S(2)}) %collective-permute-start.3) | collective-permute-done | bytes 36896 | tf_op jit(solution)/shard_map/ppermute | solution.py:260
  11.8 0.0 collective-permute-done.2
  11.9 1.6 %collective-permute-start.5 = (bf16[3,144,128]{2,1,0:T(8,128)(2,1)S(1)}, bf16[3,144,128]{2,1,0:T(8,128)(2,1)S(1)}, u32[]{:S(2)}, u32[]{:S(2)}) collective-permute-start(bf16[3,144,128]{2,1,0:T(8,128)(2,1)S(1)} %pad_maximum_fusion.3), channel_id=1, source_target_pairs={{0,2},{2,0},{1,3},{3,1},{4,6},{6,4},{5,7},{7,5},{8,10},{10,8},{9,1... | collective-permute-start | bytes 331784 | tf_op jit(solution)/shard_map/ppermute | solution.py:260
  13.4 0.1 collective-permute-start.9
  13.5 0.0 collective-permute-done.1
  13.5 3.1 %collective-permute-done.5 = bf16[3,144,128]{2,1,0:T(8,128)(2,1)S(1)} collective-permute-done((bf16[3,144,128]{2,1,0:T(8,128)(2,1)S(1)}, bf16[3,144,128]{2,1,0:T(8,128)(2,1)S(1)}, u32[]{:S(2)}, u32[]{:S(2)}) %collective-permute-start.5) | collective-permute-done | bytes 110624 | tf_op jit(solution)/shard_map/ppermute | solution.py:260
  16.7 0.0 copy-start.5
  16.7 0.0 copy-start.6
  16.7 0.1 collective-permute-start.6
  16.8 0.6 %copy-done.5 = f32[2,64]{1,0:T(2,128)S(1)} copy-done((f32[2,64]{1,0:T(2,128)S(1)}, f32[2,64]{1,0:T(2,128)}, u32[]{:S(2)}) %copy-start.5) | copy-done | bytes 536
  17.3 0.0 copy-done.6
  17.4 0.0 copy-start.1
  17.4 0.1 collective-permute-start.8
  17.5 1.1 %collective-permute-done.8.other_gains = f32[4,64]{1,0:T(4,128)S(1)} collective-permute-done((f32[4,64]{1,0:T(4,128)S(1)}, f32[4,64]{1,0:T(4,128)S(1)}, u32[]{:S(2)}, u32[]{:S(2)}) %collective-permute-start.8) | collective-permute-done | bytes 1056 | tf_op jit(solution)/shard_map/ppermute | solution.py:260
  18.6 0.0 collective-permute-done.7.other
  18.6 0.0 copy-done.1
  18.6 0.4 %shard_map.75 = (bf16[2,128,256]{2,1,0:T(8,128)(2,1)S(1)}, bf16[2,128,256]{2,1,0:T(8,128)(2,1)S(1)}, bf16[2,128,128]{2,1,0:T(8,128)(2,1)S(1)}, bf16[2,128,128]{2...) custom-call(bf16[2,6,64,128]{3,2,1,0:T(8,128)(2,1)S(1)} %pad_maximum_fusion.own, ...), custom_call_target="tpu_custom_call" | custom-call | flops 1048576 | bytes 65536 | tf_op jit(solution)/shard_map/pallas_call | solution.py:264
  19.0 0.4 %shard_map.76 = (f32[584,128]{1,0:T(8,128)S(1)}, f32[584,128]{1,0:T(8,128)S(1)}, f32[576,128]{1,0:T(8,128)S(1)}, f32[432,128]{1,0:T(8,128)S(1)}) custom-call(bf16[4,144,128]{2,1,0:T(8,128)(2,1)S(1)} %pad_maximum_fusion.2.source, f32[56,128]{1,0:T(8,128)S(1)} %get-tuple-element.27.mask, f32[4,128]{1,0:T(4,128)S(1)} %get-tuple-element.28.gains, ...), custom_call_target="tpu_custom_call" | custom-call | flops 16777216 | bytes 65536 | tf_op jit(solution)/shard_map/pallas_call | solution.py:264
  19.4 0.0 collective-permute-done.9.source
  19.4 0.4 %shard_map.77 = (f32[584,128]{1,0:T(8,128)S(1)}, f32[584,128]{1,0:T(8,128)S(1)}, f32[576,128]{1,0:T(8,128)S(1)}, f32[960,128]{1,0:T(8,128)S(1)}) custom-call(bf16[4,144,128]{2,1,0:T(8,128)(2,1)S(1)} %collective-permute-done.9.source, f32[432,128]{1,0:T(8,128)S(1)} %get-tuple-element.32.right_own, f32[56,128]{1,0:T(8,128)S(1)} %get-tuple-element.27.mask, ...), custom_call_target="tpu_custom_call" | custom-call | flops 16777216 | bytes 65536 | tf_op jit(solution)/shard_map/pallas_call | solution.py:264
  19.8 0.5 %shard_map.80 = (f32[584,128]{1,0:T(8,128)S(1)}, f32[584,128]{1,0:T(8,128)S(1)}, f32[576,128]{1,0:T(8,128)S(1)}, f32[432,128]{1,0:T(8,128)S(1)}, f32[1152,128]{1,0:T(8,128)S(1)}) custom-call(bf16[4,144,128]{2,1,0:T(8,128)(2,1)S(1)} %pad_maximum_fusion.1.source, f32[584,128]{1,0:T(8,128)S(1)} %get-tuple-element.34.near_own.near_normed_own, ...), custom_call_target="tpu_custom_call" | custom-call | flops 16777216 | bytes 65536 | tf_op jit(solution)/shard_map/pallas_call | solution.py:264
  20.3 0.8 %shard_map.78.near_tri_own = f32[960,128]{1,0:T(8,128)S(1)} custom-call(f32[576,128]{1,0:T(8,128)S(1)} %get-tuple-element.36.left, f32[960,128]{1,0:T(8,128)S(1)} %get-tuple-element.37.rightt), custom_call_target="tpu_custom_call" | custom-call | flops 33554432 | bytes 65536 | tf_op jit(solution)/shard_map/pallas_call | solution.py:264
  21.2 0.9 %shard_map.79.near_tri_other = f32[960,128]{1,0:T(8,128)S(1)} custom-call(f32[576,128]{1,0:T(8,128)S(1)} %get-tuple-element.38.left, f32[960,128]{1,0:T(8,128)S(1)} %get-tuple-element.37.rightt), custom_call_target="tpu_custom_call" | custom-call | flops 33554432 | bytes 65536 | tf_op jit(solution)/shard_map/pallas_call | solution.py:264
  22.1 0.0 collective-permute-done.6.source
  22.1 4.9 %shard_map.81 = f32[12,24,64]{2,1,0:T(8,128)} custom-call(bf16[4,144,128]{2,1,0:T(8,128)(2,1)S(1)} %collective-permute-done.6.source, f32[584,128]{1,0:T(8,128)S(1)} %get-tuple-element.31.near_raws_own, f32[584,128]{1,0:T(8,128)S(1)} %get-tuple-element.33.near_raws_other, f32[584,128]{1,0:T(8,128)S(1)} %get-tuple-element.34.near_own.near_normed_own, ...), custom_call_target="tpu_custom_call" | custom-call | flops 1048576 | bytes 65536 | tf_op jit(solution)/shard_map/pallas_call | solution.py:264
  (6 shorter events, 0.1 us)
Async XLA Ops:
  0.0 1.7 %collective-permute-start = (f32[12,24,64]{2,1,0:T(8,128)}, f32[12,24,64]{2,1,0:T(8,128)S(1)}, u32[]{:S(2)}, u32[]{:S(2)}) collective-permute-start(f32[12,24,64]{2,1,0:T(8,128)} %bitcast.16), channel_id=1, source_target_pairs={{0,1},{1,0},{2,3},{3,2},{4,5},{5,4},{6,7},{7,6},{8,9},{9,8},{10,11... | collective-permute-start | bytes 221192 | tf_op jit(solution)/shard_map/ppermute | solution.py:260
  0.5 0.9 %copy-start = (f32[64,12,24]{0,2,1:T(8,128)S(1)}, f32[64,12,24]{0,2,1:T(8,128)}, u32[]{:S(2)}) copy-start(f32[64,12,24]{0,2,1:T(8,128)} %param.7) | copy-start | bytes 221188
  1.7 5.9 %copy-start.2 = (bf16[2,4,128,64]{2,3,1,0:T(8,128)(2,1)S(1)}, bf16[2,4,128,64]{2,3,1,0:T(8,128)(2,1)}, u32[]{:S(2)}) copy-start(bf16[2,4,128,64]{2,3,1,0:T(8,128)(2,1)} %param.10) | copy-start | bytes 393220
  1.7 5.9 %copy-start.3 = (bf16[2,128,64]{1,2,0:T(8,128)(2,1)S(1)}, bf16[2,128,64]{1,2,0:T(8,128)(2,1)}, u32[]{:S(2)}) copy-start(bf16[2,128,64]{1,2,0:T(8,128)(2,1)} %param.13) | copy-start | bytes 98308
  1.7 5.9 %copy-start.4 = (bf16[2,128,64]{1,2,0:T(8,128)(2,1)S(1)}, bf16[2,128,64]{1,2,0:T(8,128)(2,1)}, u32[]{:S(2)}) copy-start(bf16[2,128,64]{1,2,0:T(8,128)(2,1)} %param.11) | copy-start | bytes 98308
  2.0 7.5 %collective-permute-start.4 = (bf16[144,128]{1,0:T(8,128)(2,1)S(1)}, bf16[144,128]{1,0:T(8,128)(2,1)S(1)}, u32[]{:S(2)}, u32[]{:S(2)}) collective-permute-start(bf16[144,128]{1,0:T(8,128)(2,1)S(1)} %shard_map.74), channel_id=1, source_target_pairs={{0,12},{4,8},{8,4},{12,0},{1,13},{5,9},{9,5},{13,1},{2,14},{6,10},... | collective-permute-start | bytes 110600 | tf_op jit(solution)/shard_map/ppermute | solution.py:260
  7.0 4.9 %collective-permute-start.3 = (bf16[144,128]{1,0:T(8,128)(2,1)S(1)}, bf16[144,128]{1,0:T(8,128)(2,1)S(1)}, u32[]{:S(2)}, u32[]{:S(2)}) collective-permute-start(bf16[144,128]{1,0:T(8,128)(2,1)S(1)} %shard_map.74), channel_id=1, source_target_pairs={{0,8},{4,12},{8,0},{12,4},{1,9},{5,13},{9,1},{13,5},{2,10},{6,14},... | collective-permute-start | bytes 110600 | tf_op jit(solution)/shard_map/ppermute | solution.py:260
  7.0 4.9 %collective-permute-start.2 = (bf16[144,128]{1,0:T(8,128)(2,1)S(1)}, bf16[144,128]{1,0:T(8,128)(2,1)S(1)}, u32[]{:S(2)}, u32[]{:S(2)}) collective-permute-start(bf16[144,128]{1,0:T(8,128)(2,1)S(1)} %shard_map.74), channel_id=1, source_target_pairs={{0,4},{4,0},{8,12},{12,8},{1,5},{5,1},{9,13},{13,9},{2,6},{6,2},{1... | collective-permute-start | bytes 110600 | tf_op jit(solution)/shard_map/ppermute | solution.py:260
  7.7 11.0 %collective-permute-start.7 = (bf16[2,6,64,128]{3,2,1,0:T(8,128)(2,1)S(1)}, bf16[2,6,64,128]{3,2,1,0:T(8,128)(2,1)S(1)}, u32[]{:S(2)}, u32[]{:S(2)}) collective-permute-start(bf16[2,6,64,128]{3,2,1,0:T(8,128)(2,1)S(1)} %pad_maximum_fusion.own), channel_id=1, source_target_pairs={{0,1},{1,0},{2,3},{3,2},{4,5},{5,4},{6,7},{7,6},{8,9},{9,8},{10,11... | collective-permute-start | bytes 589832 | tf_op jit(solution)/shard_map/ppermute | solution.py:260
  7.7 5.8 %collective-permute-start.1 = (bf16[144,128]{1,0:T(8,128)(2,1)S(1)}, bf16[144,128]{1,0:T(8,128)(2,1)S(1)}, u32[]{:S(2)}, u32[]{:S(2)}) collective-permute-start(bf16[144,128]{1,0:T(8,128)(2,1)S(1)} %shard_map.74), channel_id=1, source_target_pairs={{0,2},{2,0},{1,3},{3,1},{4,6},{6,4},{5,7},{7,5},{8,10},{10,8},{9,1... | collective-permute-start | bytes 110600 | tf_op jit(solution)/shard_map/ppermute | solution.py:260
  11.9 4.8 %collective-permute-start.5 = (bf16[3,144,128]{2,1,0:T(8,128)(2,1)S(1)}, bf16[3,144,128]{2,1,0:T(8,128)(2,1)S(1)}, u32[]{:S(2)}, u32[]{:S(2)}) collective-permute-start(bf16[3,144,128]{2,1,0:T(8,128)(2,1)S(1)} %pad_maximum_fusion.3), channel_id=1, source_target_pairs={{0,2},{2,0},{1,3},{3,1},{4,6},{6,4},{5,7},{7,5},{8,10},{10,8},{9,1... | collective-permute-start | bytes 331784 | tf_op jit(solution)/shard_map/ppermute | solution.py:260
  13.4 6.0 %collective-permute-start.9 = (bf16[4,144,128]{2,1,0:T(8,128)(2,1)S(1)}, bf16[4,144,128]{2,1,0:T(8,128)(2,1)S(1)}, u32[]{:S(2)}, u32[]{:S(2)}) collective-permute-start(bf16[4,144,128]{2,1,0:T(8,128)(2,1)S(1)} %pad_maximum_fusion.2.source), channel_id=1, source_target_pairs={{0,1},{1,0},{2,3},{3,2},{4,5},{5,4},{6,7},{7,6},{8,9},{9,8},{10,11... | collective-permute-start | bytes 442376 | tf_op jit(solution)/shard_map/ppermute | solution.py:260
  16.7 0.7 %copy-start.5 = (f32[2,64]{1,0:T(2,128)S(1)}, f32[2,64]{1,0:T(2,128)}, u32[]{:S(2)}) copy-start(f32[2,64]{1,0:T(2,128)} %param.12) | copy-start | bytes 1540
  16.7 0.7 %copy-start.6 = (f32[2,64]{1,0:T(2,128)S(1)}, f32[2,64]{1,0:T(2,128)}, u32[]{:S(2)}) copy-start(f32[2,64]{1,0:T(2,128)} %param.9) | copy-start | bytes 1540
  16.7 5.4 %collective-permute-start.6 = (bf16[4,144,128]{2,1,0:T(8,128)(2,1)S(1)}, bf16[4,144,128]{2,1,0:T(8,128)(2,1)S(1)}, u32[]{:S(2)}, u32[]{:S(2)}) collective-permute-start(bf16[4,144,128]{2,1,0:T(8,128)(2,1)S(1)} %pad_maximum_fusion.1.source), channel_id=1, source_target_pairs={{0,1},{1,0},{2,3},{3,2},{4,5},{5,4},{6,7},{7,6},{8,9},{9,8},{10,11... | collective-permute-start | bytes 442376 | tf_op jit(solution)/shard_map/ppermute | solution.py:260
  17.4 1.2 %copy-start.1 = (s32[48]{0:T(128)S(1)}, s32[48]{0:T(128)}, u32[]{:S(2)}) copy-start(s32[48]{0:T(128)} %param.8) | copy-start | bytes 580
  17.4 1.2 %collective-permute-start.8 = (f32[4,64]{1,0:T(4,128)S(1)}, f32[4,64]{1,0:T(4,128)S(1)}, u32[]{:S(2)}, u32[]{:S(2)}) collective-permute-start(f32[4,64]{1,0:T(4,128)S(1)} %pad_maximum_fusion.4.own_gains), channel_id=1, source_target_pairs={{0,1},{1,0},{2,3},{3,2},{4,5},{5,4},{6,7},{7,6},{8,9},{9,8},{10,11... | collective-permute-start | bytes 3080 | tf_op jit(solution)/shard_map/ppermute | solution.py:260

commit v5 on v4

--- a/solution.py
+++ b/solution.py
@@ -315,8 +315,13 @@
     )
     near = jnp.stack(column)
     far_first = swap(message, "gy")
-    far_rest = swap(jnp.stack(column[1:]), "gy")
-    far = jnp.concatenate([far_first[None], far_rest], axis=0)
+    early = 2 % blocks
+    far_second = swap(column[early], "gy")
+    rest = [s for s in range(1, blocks) if s != early]
+    far_rest = swap(jnp.stack([column[s] for s in rest]), "gy")
+    arrived = {0: far_first, early: far_second}
+    arrived.update({s: far_rest[n] for n, s in enumerate(rest)})
+    far = jnp.stack([arrived[s] for s in range(blocks)])
     near_other = swap(near, "gz")
     far_other = swap(far, "gz")
     part_pairs = pairs // 2
@@ -456,6 +461,7 @@
         and res * res * part * 2 * 4 <= REPLICATED_LIMIT
         and lax.axis_size("gy") == 2
         and lax.axis_size("gx").bit_count() == 1
+        and lax.axis_size("gx") >= 4
         and res % 8 == 0
         and res // tile_rows * (tile_rows // 2) % 4 == 0
         and tile_rows % 2 == 0

time: 27.2 us -> 27.2 us (level)
  starting transfers between devices: 9.69 us -> 10.8 us
  waiting for transfers between devices: 6.99 us -> 5.88 us
    ppermute x10 -> x11, waiting for transfers between devices: 6.99 us -> 5.88 us  [swap(): return lax.ppermute(x, axis, [(i, i ^ mask) for i in range(size)])]
    ppermute x10 -> x11, starting transfers between devices: 9.69 us -> 10.8 us  [swap(): return lax.ppermute(x, axis, [(i, i ^ mask) for i in range(size)])]
  transfers between devices with their start and end apart: 10 -> 11, of which waited for: 4 -> 5; matrix products, arithmetic and copies ran while one was open for 0% -> 0% of each run, Pallas kernels for 13% -> 13%
where the time goes in v5:
time: 27.2 us; the launch traced here: 27 us
  starting transfers between devices  10.8 us (40%)
  Pallas kernels  8.62 us (32%)
  waiting for transfers between devices  5.88 us (22%)
  local copies, waits for them, and re-layouts  1.52 us (6%)
    ppermute x11, starting transfers between devices, swap(): return lax.ppermute(x, axis, [(i, i ^ mask) for i in range(size)])  10.8 us
    pallas_call x9, Pallas kernels, call(): pl.pallas_call(kernel, out_shape=out_shape, scratch_shapes=list(scratch),...  8.62 us
    ppermute x11, waiting for transfers between devices, swap(): return lax.ppermute(x, axis, [(i, i ^ mask) for i in range(size)])  5.88 us
    unnamed x14, local copies, waits for them, and re-layouts  1.51 us
  transfers between devices with their start and end apart: 11, of which 5 were waited for; matrix products, arithmetic and copies ran while one was open for 0% of the time, Pallas kernels for 13%

profile of v5, /device:TPU:0, one launch (start us, length us, event | category | flops | bytes accessed | tf_op | source)
XLA Modules:
  0.0 27.0 jit_solution(14467406085728287790)
XLA Ops:
  0.0 0.5 %collective-permute-start = (f32[12,24,64]{2,1,0:T(8,128)}, f32[12,24,64]{2,1,0:T(8,128)S(1)}, u32[]{:S(2)}, u32[]{:S(2)}) collective-permute-start(f32[12,24,64]{2,1,0:T(8,128)} %bitcast.17), channel_id=1, source_target_pairs={{0,1},{1,0},{2,3},{3,2},{4,5},{5,4},{6,7},{7,6},{8,9},{9,8},{10,11... | collective-permute-start | bytes 221192 | tf_op jit(solution)/shard_map/ppermute | solution.py:260
  0.5 0.0 copy-start
  0.5 0.9 %copy-done = f32[64,12,24]{0,2,1:T(8,128)S(1)} copy-done((f32[64,12,24]{0,2,1:T(8,128)S(1)}, f32[64,12,24]{0,2,1:T(8,128)}, u32[]{:S(2)}) %copy-start) | copy-done | bytes 73752
  1.4 0.3 %collective-permute-done.other = f32[12,24,64]{2,1,0:T(8,128)S(1)} collective-permute-done((f32[12,24,64]{2,1,0:T(8,128)}, f32[12,24,64]{2,1,0:T(8,128)S(1)}, u32[]{:S(2)}, u32[]{:S(2)}) %collective-permute-start) | collective-permute-done | bytes 73760 | tf_op jit(solution)/shard_map/ppermute | solution.py:260
  1.7 0.0 copy-start.2
  1.7 0.0 copy-start.3
  1.7 0.0 copy-start.4
  1.7 0.2 shard_map.74
  2.0 5.0 %collective-permute-start.3 = (bf16[144,128]{1,0:T(8,128)(2,1)S(1)}, bf16[144,128]{1,0:T(8,128)(2,1)S(1)}, u32[]{:S(2)}, u32[]{:S(2)}) collective-permute-start(bf16[144,128]{1,0:T(8,128)(2,1)S(1)} %shard_map.74), channel_id=1, source_target_pairs={{0,12},{4,8},{8,4},{12,0},{1,13},{5,9},{9,5},{13,1},{2,14},{6,10},... | collective-permute-start | bytes 110600 | tf_op jit(solution)/shard_map/ppermute | solution.py:260
  7.0 0.0 collective-permute-start.2
  7.0 0.0 copy-done.2
  7.0 0.0 copy-done.3
  7.0 0.0 copy-done.4
  7.0 0.1 collective-permute-start.8
  7.1 0.7 %collective-permute-start.5 = (bf16[144,128]{1,0:T(8,128)(2,1)S(1)}, bf16[144,128]{1,0:T(8,128)(2,1)S(1)}, u32[]{:S(2)}, u32[]{:S(2)}) collective-permute-start(bf16[144,128]{1,0:T(8,128)(2,1)S(1)} %shard_map.74), channel_id=1, source_target_pairs={{0,8},{4,12},{8,0},{12,4},{1,9},{5,13},{9,1},{13,5},{2,10},{6,14},... | collective-permute-start | bytes 110600 | tf_op jit(solution)/shard_map/ppermute | solution.py:260
  7.8 1.6 %collective-permute-start.1 = (bf16[144,128]{1,0:T(8,128)(2,1)S(1)}, bf16[144,128]{1,0:T(8,128)(2,1)S(1)}, u32[]{:S(2)}, u32[]{:S(2)}) collective-permute-start(bf16[144,128]{1,0:T(8,128)(2,1)S(1)} %shard_map.74), channel_id=1, source_target_pairs={{0,2},{2,0},{1,3},{3,1},{4,6},{6,4},{5,7},{7,5},{8,10},{10,8},{9,1... | collective-permute-start | bytes 110600 | tf_op jit(solution)/shard_map/ppermute | solution.py:260
  9.4 0.0 collective-permute-done.3
  9.4 1.5 %collective-permute-done.2 = bf16[144,128]{1,0:T(8,128)(2,1)S(1)} collective-permute-done((bf16[144,128]{1,0:T(8,128)(2,1)S(1)}, bf16[144,128]{1,0:T(8,128)(2,1)S(1)}, u32[]{:S(2)}, u32[]{:S(2)}) %collective-permute-start.2) | collective-permute-done | bytes 36896 | tf_op jit(solution)/shard_map/ppermute | solution.py:260
  10.9 1.6 %collective-permute-start.4 = (bf16[2,144,128]{2,1,0:T(8,128)(2,1)S(1)}, bf16[2,144,128]{2,1,0:T(8,128)(2,1)S(1)}, u32[]{:S(2)}, u32[]{:S(2)}) collective-permute-start(bf16[2,144,128]{2,1,0:T(8,128)(2,1)S(1)} %pad_maximum_fusion.3), channel_id=1, source_target_pairs={{0,2},{2,0},{1,3},{3,1},{4,6},{6,4},{5,7},{7,5},{8,10},{10,8},{9,1... | collective-permute-start | bytes 221192 | tf_op jit(solution)/shard_map/ppermute | solution.py:260
  12.5 0.0 collective-permute-done.5
  12.5 0.1 collective-permute-start.10
  12.6 1.1 %collective-permute-start.6 = (bf16[144,128]{1,0:T(8,128)(2,1)S(1)}, bf16[144,128]{1,0:T(8,128)(2,1)S(1)}, u32[]{:S(2)}, u32[]{:S(2)}) collective-permute-start(bf16[144,128]{1,0:T(8,128)(2,1)S(1)} %collective-permute-done.5), channel_id=1, source_target_pairs={{0,2},{2,0},{1,3},{3,1},{4,6},{6,4},{5,7},{7,5},{8,10},{10,8},{9,1... | collective-permute-start | bytes 110600 | tf_op jit(solution)/shard_map/ppermute | solution.py:260
  13.7 1.7 %collective-permute-done.4 = bf16[2,144,128]{2,1,0:T(8,128)(2,1)S(1)} collective-permute-done((bf16[2,144,128]{2,1,0:T(8,128)(2,1)S(1)}, bf16[2,144,128]{2,1,0:T(8,128)(2,1)S(1)}, u32[]{:S(2)}, u32[]{:S(2)}) %collective-permute-start.4) | collective-permute-done | bytes 73760 | tf_op jit(solution)/shard_map/ppermute | solution.py:260
  15.4 0.0 collective-permute-done.1
  15.4 1.3 %collective-permute-done.6 = bf16[144,128]{1,0:T(8,128)(2,1)S(1)} collective-permute-done((bf16[144,128]{1,0:T(8,128)(2,1)S(1)}, bf16[144,128]{1,0:T(8,128)(2,1)S(1)}, u32[]{:S(2)}, u32[]{:S(2)}) %collective-permute-start.6) | collective-permute-done | bytes 36896 | tf_op jit(solution)/shard_map/ppermute | solution.py:260
  16.6 0.0 copy-start.5
  16.6 0.0 copy-start.6
  16.7 0.1 collective-permute-start.7
  16.7 0.6 %copy-done.5 = f32[2,64]{1,0:T(2,128)S(1)} copy-done((f32[2,64]{1,0:T(2,128)S(1)}, f32[2,64]{1,0:T(2,128)}, u32[]{:S(2)}) %copy-start.5) | copy-done | bytes 536
  17.3 0.0 copy-done.6
  17.3 0.0 copy-start.1
  17.3 0.1 collective-permute-start.9
  17.4 1.1 %collective-permute-done.9.other_gains = f32[4,64]{1,0:T(4,128)S(1)} collective-permute-done((f32[4,64]{1,0:T(4,128)S(1)}, f32[4,64]{1,0:T(4,128)S(1)}, u32[]{:S(2)}, u32[]{:S(2)}) %collective-permute-start.9) | collective-permute-done | bytes 1056 | tf_op jit(solution)/shard_map/ppermute | solution.py:260
  18.6 0.0 collective-permute-done.8.other
  18.6 0.0 copy-done.1
  18.6 0.4 %shard_map.75 = (bf16[2,128,256]{2,1,0:T(8,128)(2,1)S(1)}, bf16[2,128,256]{2,1,0:T(8,128)(2,1)S(1)}, bf16[2,128,128]{2,1,0:T(8,128)(2,1)S(1)}, bf16[2,128,128]{2...) custom-call(bf16[2,6,64,128]{3,2,1,0:T(8,128)(2,1)S(1)} %pad_maximum_fusion.own, ...), custom_call_target="tpu_custom_call" | custom-call | flops 1048576 | bytes 65536 | tf_op jit(solution)/shard_map/pallas_call | solution.py:264
  18.9 0.4 %shard_map.76 = (f32[584,128]{1,0:T(8,128)S(1)}, f32[584,128]{1,0:T(8,128)S(1)}, f32[576,128]{1,0:T(8,128)S(1)}, f32[432,128]{1,0:T(8,128)S(1)}) custom-call(bf16[4,144,128]{2,1,0:T(8,128)(2,1)S(1)} %pad_maximum_fusion.2.source, f32[56,128]{1,0:T(8,128)S(1)} %get-tuple-element.27.mask, f32[4,128]{1,0:T(4,128)S(1)} %get-tuple-element.28.gains, ...), custom_call_target="tpu_custom_call" | custom-call | flops 16777216 | bytes 65536 | tf_op jit(solution)/shard_map/pallas_call | solution.py:264
  19.4 0.0 collective-permute-done.10.source
  19.4 0.4 %shard_map.77 = (f32[584,128]{1,0:T(8,128)S(1)}, f32[584,128]{1,0:T(8,128)S(1)}, f32[576,128]{1,0:T(8,128)S(1)}, f32[960,128]{1,0:T(8,128)S(1)}) custom-call(bf16[4,144,128]{2,1,0:T(8,128)(2,1)S(1)} %collective-permute-done.10.source, f32[432,128]{1,0:T(8,128)S(1)} %get-tuple-element.32.right_own, f32[56,128]{1,0:T(8,128)S(1)} %get-tuple-element.27.mask, ...), custom_call_target="tpu_custom_call" | custom-call | flops 16777216 | bytes 65536 | tf_op jit(solution)/shard_map/pallas_call | solution.py:264
  19.8 0.5 %shard_map.80 = (f32[584,128]{1,0:T(8,128)S(1)}, f32[584,128]{1,0:T(8,128)S(1)}, f32[576,128]{1,0:T(8,128)S(1)}, f32[432,128]{1,0:T(8,128)S(1)}, f32[1152,128]{1,0:T(8,128)S(1)}) custom-call(bf16[4,144,128]{2,1,0:T(8,128)(2,1)S(1)} %pad_maximum_fusion.1.source, f32[584,128]{1,0:T(8,128)S(1)} %get-tuple-element.34.near_own.near_normed_own, ...), custom_call_target="tpu_custom_call" | custom-call | flops 16777216 | bytes 65536 | tf_op jit(solution)/shard_map/pallas_call | solution.py:264
  20.3 0.8 %shard_map.78.near_tri_own = f32[960,128]{1,0:T(8,128)S(1)} custom-call(f32[576,128]{1,0:T(8,128)S(1)} %get-tuple-element.36.left, f32[960,128]{1,0:T(8,128)S(1)} %get-tuple-element.37.rightt), custom_call_target="tpu_custom_call" | custom-call | flops 33554432 | bytes 65536 | tf_op jit(solution)/shard_map/pallas_call | solution.py:264
  21.1 0.9 %shard_map.79.near_tri_other = f32[960,128]{1,0:T(8,128)S(1)} custom-call(f32[576,128]{1,0:T(8,128)S(1)} %get-tuple-element.38.left, f32[960,128]{1,0:T(8,128)S(1)} %get-tuple-element.37.rightt), custom_call_target="tpu_custom_call" | custom-call | flops 33554432 | bytes 65536 | tf_op jit(solution)/shard_map/pallas_call | solution.py:264
  22.1 0.0 collective-permute-done.7.source
  22.1 4.9 %shard_map.81 = f32[12,24,64]{2,1,0:T(8,128)} custom-call(bf16[4,144,128]{2,1,0:T(8,128)(2,1)S(1)} %collective-permute-done.7.source, f32[584,128]{1,0:T(8,128)S(1)} %get-tuple-element.31.near_raws_own, f32[584,128]{1,0:T(8,128)S(1)} %get-tuple-element.33.near_raws_other, f32[584,128]{1,0:T(8,128)S(1)} %get-tuple-element.34.near_own.near_normed_own, ...), custom_call_target="tpu_custom_call" | custom-call | flops 1048576 | bytes 65536 | tf_op jit(solution)/shard_map/pallas_call | solution.py:264
  (7 shorter events, 0.1 us)
Async XLA Ops:
  0.0 1.7 %collective-permute-start = (f32[12,24,64]{2,1,0:T(8,128)}, f32[12,24,64]{2,1,0:T(8,128)S(1)}, u32[]{:S(2)}, u32[]{:S(2)}) collective-permute-start(f32[12,24,64]{2,1,0:T(8,128)} %bitcast.17), channel_id=1, source_target_pairs={{0,1},{1,0},{2,3},{3,2},{4,5},{5,4},{6,7},{7,6},{8,9},{9,8},{10,11... | collective-permute-start | bytes 221192 | tf_op jit(solution)/shard_map/ppermute | solution.py:260
  0.5 0.9 %copy-start = (f32[64,12,24]{0,2,1:T(8,128)S(1)}, f32[64,12,24]{0,2,1:T(8,128)}, u32[]{:S(2)}) copy-start(f32[64,12,24]{0,2,1:T(8,128)} %param.7) | copy-start | bytes 221188
  1.7 5.3 %copy-start.2 = (bf16[2,4,128,64]{2,3,1,0:T(8,128)(2,1)S(1)}, bf16[2,4,128,64]{2,3,1,0:T(8,128)(2,1)}, u32[]{:S(2)}) copy-start(bf16[2,4,128,64]{2,3,1,0:T(8,128)(2,1)} %param.10) | copy-start | bytes 393220
  1.7 5.3 %copy-start.3 = (bf16[2,128,64]{1,2,0:T(8,128)(2,1)S(1)}, bf16[2,128,64]{1,2,0:T(8,128)(2,1)}, u32[]{:S(2)}) copy-start(bf16[2,128,64]{1,2,0:T(8,128)(2,1)} %param.13) | copy-start | bytes 98308
  1.7 5.3 %copy-start.4 = (bf16[2,128,64]{1,2,0:T(8,128)(2,1)S(1)}, bf16[2,128,64]{1,2,0:T(8,128)(2,1)}, u32[]{:S(2)}) copy-start(bf16[2,128,64]{1,2,0:T(8,128)(2,1)} %param.11) | copy-start | bytes 98308
  2.0 7.5 %collective-permute-start.3 = (bf16[144,128]{1,0:T(8,128)(2,1)S(1)}, bf16[144,128]{1,0:T(8,128)(2,1)S(1)}, u32[]{:S(2)}, u32[]{:S(2)}) collective-permute-start(bf16[144,128]{1,0:T(8,128)(2,1)S(1)} %shard_map.74), channel_id=1, source_target_pairs={{0,12},{4,8},{8,4},{12,0},{1,13},{5,9},{9,5},{13,1},{2,14},{6,10},... | collective-permute-start | bytes 110600 | tf_op jit(solution)/shard_map/ppermute | solution.py:260
  7.0 4.0 %collective-permute-start.2 = (bf16[144,128]{1,0:T(8,128)(2,1)S(1)}, bf16[144,128]{1,0:T(8,128)(2,1)S(1)}, u32[]{:S(2)}, u32[]{:S(2)}) collective-permute-start(bf16[144,128]{1,0:T(8,128)(2,1)S(1)} %shard_map.74), channel_id=1, source_target_pairs={{0,4},{4,0},{8,12},{12,8},{1,5},{5,1},{9,13},{13,9},{2,6},{6,2},{1... | collective-permute-start | bytes 110600 | tf_op jit(solution)/shard_map/ppermute | solution.py:260
  7.0 11.5 %collective-permute-start.8 = (bf16[2,6,64,128]{3,2,1,0:T(8,128)(2,1)S(1)}, bf16[2,6,64,128]{3,2,1,0:T(8,128)(2,1)S(1)}, u32[]{:S(2)}, u32[]{:S(2)}) collective-permute-start(bf16[2,6,64,128]{3,2,1,0:T(8,128)(2,1)S(1)} %pad_maximum_fusion.own), channel_id=1, source_target_pairs={{0,1},{1,0},{2,3},{3,2},{4,5},{5,4},{6,7},{7,6},{8,9},{9,8},{10,11... | collective-permute-start | bytes 589832 | tf_op jit(solution)/shard_map/ppermute | solution.py:260
  7.1 5.4 %collective-permute-start.5 = (bf16[144,128]{1,0:T(8,128)(2,1)S(1)}, bf16[144,128]{1,0:T(8,128)(2,1)S(1)}, u32[]{:S(2)}, u32[]{:S(2)}) collective-permute-start(bf16[144,128]{1,0:T(8,128)(2,1)S(1)} %shard_map.74), channel_id=1, source_target_pairs={{0,8},{4,12},{8,0},{12,4},{1,9},{5,13},{9,1},{13,5},{2,10},{6,14},... | collective-permute-start | bytes 110600 | tf_op jit(solution)/shard_map/ppermute | solution.py:260
  7.8 7.6 %collective-permute-start.1 = (bf16[144,128]{1,0:T(8,128)(2,1)S(1)}, bf16[144,128]{1,0:T(8,128)(2,1)S(1)}, u32[]{:S(2)}, u32[]{:S(2)}) collective-permute-start(bf16[144,128]{1,0:T(8,128)(2,1)S(1)} %shard_map.74), channel_id=1, source_target_pairs={{0,2},{2,0},{1,3},{3,1},{4,6},{6,4},{5,7},{7,5},{8,10},{10,8},{9,1... | collective-permute-start | bytes 110600 | tf_op jit(solution)/shard_map/ppermute | solution.py:260
  10.9 4.4 %collective-permute-start.4 = (bf16[2,144,128]{2,1,0:T(8,128)(2,1)S(1)}, bf16[2,144,128]{2,1,0:T(8,128)(2,1)S(1)}, u32[]{:S(2)}, u32[]{:S(2)}) collective-permute-start(bf16[2,144,128]{2,1,0:T(8,128)(2,1)S(1)} %pad_maximum_fusion.3), channel_id=1, source_target_pairs={{0,2},{2,0},{1,3},{3,1},{4,6},{6,4},{5,7},{7,5},{8,10},{10,8},{9,1... | collective-permute-start | bytes 221192 | tf_op jit(solution)/shard_map/ppermute | solution.py:260
  12.5 6.8 %collective-permute-start.10 = (bf16[4,144,128]{2,1,0:T(8,128)(2,1)S(1)}, bf16[4,144,128]{2,1,0:T(8,128)(2,1)S(1)}, u32[]{:S(2)}, u32[]{:S(2)}) collective-permute-start(bf16[4,144,128]{2,1,0:T(8,128)(2,1)S(1)} %pad_maximum_fusion.2.source), channel_id=1, source_target_pairs={{0,1},{1,0},{2,3},{3,2},{4,5},{5,4},{6,7},{7,6},{8,9},{9,8},{10,11... | collective-permute-start | bytes 442376 | tf_op jit(solution)/shard_map/ppermute | solution.py:260
  12.6 4.0 %collective-permute-start.6 = (bf16[144,128]{1,0:T(8,128)(2,1)S(1)}, bf16[144,128]{1,0:T(8,128)(2,1)S(1)}, u32[]{:S(2)}, u32[]{:S(2)}) collective-permute-start(bf16[144,128]{1,0:T(8,128)(2,1)S(1)} %collective-permute-done.5), channel_id=1, source_target_pairs={{0,2},{2,0},{1,3},{3,1},{4,6},{6,4},{5,7},{7,5},{8,10},{10,8},{9,1... | collective-permute-start | bytes 110600 | tf_op jit(solution)/shard_map/ppermute | solution.py:260
  16.6 0.7 %copy-start.5 = (f32[2,64]{1,0:T(2,128)S(1)}, f32[2,64]{1,0:T(2,128)}, u32[]{:S(2)}) copy-start(f32[2,64]{1,0:T(2,128)} %param.12) | copy-start | bytes 1540
  16.6 0.7 %copy-start.6 = (f32[2,64]{1,0:T(2,128)S(1)}, f32[2,64]{1,0:T(2,128)}, u32[]{:S(2)}) copy-start(f32[2,64]{1,0:T(2,128)} %param.9) | copy-start | bytes 1540
  16.7 5.4 %collective-permute-start.7 = (bf16[4,144,128]{2,1,0:T(8,128)(2,1)S(1)}, bf16[4,144,128]{2,1,0:T(8,128)(2,1)S(1)}, u32[]{:S(2)}, u32[]{:S(2)}) collective-permute-start(bf16[4,144,128]{2,1,0:T(8,128)(2,1)S(1)} %pad_maximum_fusion.1.source), channel_id=1, source_target_pairs={{0,1},{1,0},{2,3},{3,2},{4,5},{5,4},{6,7},{7,6},{8,9},{9,8},{10,11... | collective-permute-start | bytes 442376 | tf_op jit(solution)/shard_map/ppermute | solution.py:260
  17.3 1.2 %copy-start.1 = (s32[48]{0:T(128)S(1)}, s32[48]{0:T(128)}, u32[]{:S(2)}) copy-start(s32[48]{0:T(128)} %param.8) | copy-start | bytes 580
  17.3 1.2 %collective-permute-start.9 = (f32[4,64]{1,0:T(4,128)S(1)}, f32[4,64]{1,0:T(4,128)S(1)}, u32[]{:S(2)}, u32[]{:S(2)}) collective-permute-start(f32[4,64]{1,0:T(4,128)S(1)} %pad_maximum_fusion.4.own_gains), channel_id=1, source_target_pairs={{0,1},{1,0},{2,3},{3,2},{4,5},{5,4},{6,7},{7,6},{8,9},{9,8},{10,11... | collective-permute-start | bytes 3080 | tf_op jit(solution)/shard_map/ppermute | solution.py:260
